TPU v7x, 16 devices: a 4x2x1 block of a 4x4x8 slice. The times are simulated.
16 devices in a mesh: req: 2 (over y, z), cp: 8 (over x, core).
Axes of the slice: x: 4, y: 2, z: 1, core: 2. Of those that a mesh axis runs over, the one named last changes fastest.
The devices are a block of a 4x4x8 slice.
Arguments:
- x: bfloat16 [12288, 2048], P(('req', 'cp')), parts along dimension 0
- pos: int32 [12288], P(('req', 'cp')), parts along dimension 0
- g1: bfloat16 [2, 2048], replicated
- g2: bfloat16 [2, 2048], replicated
- wq: bfloat16 [2, 2048, 2048], replicated
- wk: bfloat16 [2, 2048, 2048], replicated
- wv: bfloat16 [2, 2048, 2048], replicated
- wo: bfloat16 [2, 2048, 2048], replicated
- w1: bfloat16 [2, 2048, 8192], replicated
- w3: bfloat16 [2, 2048, 8192], replicated
- w2: bfloat16 [2, 8192, 2048], replicated
Outputs:
- output 1: bfloat16 [12288, 2048], P(('req', 'cp')), parts along dimension 0
- output 2: bfloat16 [2, 12288, 16, 128], P(None, 'req', 'cp'), parts along dimension 1
- output 3: bfloat16 [2, 12288, 16, 128], P(None, 'req', 'cp'), parts along dimension 1
There are 2 independent parts. A program takes and returns all parts, laid end to end along the dimension named above; an argument that names none is the same for every part.
All inputs are finite; a program needn't handle non-finite values.
Results may differ from a plain program's by a relative error of at most 0.0178628.
Values are sent between devices in bfloat16 or wider.
A program may use at most 768 MiB of HBM per device.

v0:
```python
import jax
import jax.numpy as jnp
from jax import lax
from jax.sharding import PartitionSpec as P

HEAD = 128
F32 = jnp.float32
BF16 = jnp.bfloat16


def _norm(x, g):
    x32 = x.astype(F32)
    r = lax.rsqrt(jnp.mean(x32 * x32, axis=-1, keepdims=True) + 1e-5)
    return (x32 * r * g.astype(F32)).astype(BF16)


def _angles(pos):
    half = HEAD // 2
    inv = 1.0 / (10000.0 ** (jnp.arange(half, dtype=F32) * (2.0 / HEAD)))
    ang = pos.astype(F32)[..., None] * inv
    return jnp.cos(ang)[..., None, :], jnp.sin(ang)[..., None, :]


def _rope(t, c, sn):
    half = HEAD // 2
    t1, t2 = t[..., :half], t[..., half:]
    return jnp.concatenate([t1 * c - t2 * sn, t2 * c + t1 * sn], axis=-1)


def _attention(q, kg, vg, mask):
    def one(a):
        qh, kh, vh = a
        sc = jnp.einsum('qd,kd->qk', qh, kh, preferred_element_type=F32) * HEAD ** -0.5
        p = jax.nn.softmax(jnp.where(mask, sc, -jnp.inf), axis=-1).astype(BF16)
        return jnp.dot(p, vh, preferred_element_type=F32).astype(BF16)

    o = lax.map(one, (q.transpose(1, 0, 2), kg.transpose(1, 0, 2), vg.transpose(1, 0, 2)))
    return o.transpose(1, 0, 2).reshape(q.shape[0], -1)


def _natural(a, ncp):
    n, seq = a.shape[0], a.shape[1]
    a = a.reshape((n, ncp, 2, seq // (2 * ncp)) + a.shape[2:])
    a = jnp.concatenate([a[:, :, 0], a[:, ::-1, 1]], axis=1)
    return a.reshape((n, seq) + a.shape[3:])


def solution(mesh):
    ncp = mesh.shape['cp']
    act = P(('req', 'cp'), None)
    cache = P(None, 'req', 'cp', None)

    def body(x, pos, g1, g2, wq, wk, wv, wo, w1, w3, w2):
        s_dev = x.shape[0]
        nh = wq.shape[2] // HEAD
        pos_all = lax.all_gather(pos, 'cp', tiled=True)
        mask = pos_all[None, :] <= pos[:, None]
        c, sn = _angles(pos)
        kl, vl = [], []
        for l in range(wq.shape[0]):
            h = _norm(x, g1[l])
            q = _rope(jnp.dot(h, wq[l], preferred_element_type=F32).reshape(s_dev, nh, HEAD), c, sn).astype(BF16)
            k = _rope(jnp.dot(h, wk[l], preferred_element_type=F32).reshape(s_dev, nh, HEAD), c, sn).astype(BF16)
            v = jnp.dot(h, wv[l], preferred_element_type=F32).astype(BF16).reshape(s_dev, nh, HEAD)
            kg = lax.all_gather(k, 'cp', tiled=True)
            vg = lax.all_gather(v, 'cp', tiled=True)
            o = _attention(q, kg, vg, mask)
            x = (x.astype(F32) + jnp.dot(o, wo[l], preferred_element_type=F32)).astype(BF16)
            h2 = _norm(x, g2[l])
            u = (jax.nn.silu(jnp.dot(h2, w1[l], preferred_element_type=F32))
                 * jnp.dot(h2, w3[l], preferred_element_type=F32)).astype(BF16)
            x = (x.astype(F32) + jnp.dot(u, w2[l], preferred_element_type=F32)).astype(BF16)
            kl.append(k)
            vl.append(v)
        kc = _natural(lax.all_to_all(jnp.stack(kl), 'cp', 2, 1, tiled=True), ncp)
        vc = _natural(lax.all_to_all(jnp.stack(vl), 'cp', 2, 1, tiled=True), ncp)
        return x, kc, vc

    return jax.shard_map(body, mesh=mesh, in_specs=(act, P(('req', 'cp'))) + (P(),) * 9,
                         out_specs=(act, cache, cache), check_vma=False)
```

profile of v0, /device:TPU:112, one launch (start us, length us, event | category | flops | bytes accessed | tf_op | source)
XLA Modules:
  0.0 1980.9 jit_solution(14578312069520891523)
XLA Ops:
  11.2 12.0 slice_bitcast_fusion
  23.2 12.3 copy.61
  47.5 12.5 copy.60
  83.1 20.9 %fusion.106 = bf16[768,2048]{1,0:T(8,128)(2,1)S(1)} fusion(bf16[2,2048,2048]{2,1,0:T(8,128)(2,1)} %param.21, bf16[768,2048]{1,0:T(8,128)(2,1)} %param.15, f32[2048]{0:T(1024)S(1)} %bitcast.256, f32[768]{0:T(1024)S(1)} %add_rsqrt_fusion.3), kind=kOutput, calls=%fused_computation.110 | convolution fusion | flops 6450315264 | bytes 14691328 | tf_op jit(solution)/shard_map/dot_general | solution.py:64
  108.3 24.7 %all-gather = s32[8,1,768]{2,1,0:T(1,128)} all-gather(s32[1,1,768]{2,1,0:T(1,128)S(1)} %reshape.203), channel_id=1, replica_groups=mesh['req'=2,'cp'=8] {'cp'}, dimensions={0}, use_global_device_ids=true | all-gather | bytes 27648 | tf_op jit(solution)/shard_map/all_gather | solution.py:56
  135.5 68.0 %all-gather.6.cloned.1.call-done = bf16[6144,16,128]{0,2,1:T(8,128)(2,1)} async-done(((bf16[768,16,128]{0,2,1:T(8,128)(2,1)}), bf16[6144,16,128]{0,2,1:T(8,128)(2,1)}) %all-gather.6.cloned.1.call-update) | async-done | bytes 25165840 | tf_op jit(solution)/shard_map/all_gather | solution.py:65
  203.5 119.8 %all-gather.8.cloned.1.call-done = bf16[6144,16,128]{2,0,1:T(8,128)(2,1)} async-done(((bf16[768,16,128]{2,0,1:T(8,128)(2,1)}), bf16[6144,16,128]{2,0,1:T(8,128)(2,1)}) %all-gather.8.cloned.1.call-update) | async-done | bytes 25165840 | tf_op jit(solution)/shard_map/all_gather | solution.py:66
  325.2 508.3 %while.22 = (s32[]{:T(128)}, bf16[16,768,128]{1,2,0:T(8,128)(2,1)}, bf16[16,768,128]{1,2,0:T(8,128)(2,1)}, bf16[16,6144,128]{1,2,0:T(8,128)(2,1)}, bf16[16,6144,...) while((s32[]{:T(128)}, bf16[16,768,128]{1,2,0:T(8,128)(2,1)}, ...), condition=%wide.region_4.5_spmd.clone, body=%wide.region_1.4_spmd.clone.sunk | while | flops 2486794752 | bytes 61048916 | solution.py:37
  846.1 33.1 %fusion.54 = f32[768,8192]{1,0:T(8,128)} fusion(bf16[2,2048,8192]{2,1,0:T(8,128)(2,1)} %param.23, bf16[768,2048]{1,0:T(8,128)(2,1)S(1)} %get-tuple-element.224, f32[2048]{0:T(1024)S(1)} %bitcast.252, f32[768]{0:T(1024)S(1)} %add_rsqrt_fusion.2), kind=kOutput, calls=%fused_computation.52 | convolution fusion | flops 25776095232 | bytes 61877248 | tf_op jit(solution)/shard_map/dot_general | solution.py:70
  879.2 36.4 %multiply_convert_fusion.1.clone.1.clone.5 = bf16[768,8192]{1,0:T(8,128)(2,1)} fusion(f32[768,8192]{1,0:T(8,128)} %fusion.54, bf16[2,2048,8192]{2,1,0:T(8,128)(2,1)} %param.24, bf16[768,2048]{1,0:T(8,128)(2,1)} %copy-done.28, f32[2048]{0:T(1024)S(1)} %bitcast.253, f32[768]{0:T(1024)S(1)} %add_rsqrt_fusion.2), kind=kOutput, calls=%fused_computation.61.clone.clone.clone.clone.clone.2 | convolution fusion | flops 25813843968 | bytes 74460160 | tf_op jit(solution)/shard_map/dot_general | solution.py:71
  915.6 34.3 %fusion.86 = (f32[768]{0:T(1024)S(1)}, bf16[768,2048]{1,0:T(8,128)(2,1)S(1)}) fusion(bf16[2,8192,2048]{2,1,0:T(8,128)(2,1)} %param.25, bf16[768,2048]{1,0:T(8,128)(2,1)} %copy-done.28, bf16[768,8192]{1,0:T(8,128)(2,1)} %multiply_convert_fusion.1.clone.1.clone.5), kind=kOutput, calls=%fused_computation.98 | convolution fusion | flops 25779240960 | bytes 52431872 | tf_op jit(solution)/shard_map/dot_general | solution.py:72
  964.7 12.3 copy.66
  977.0 12.4 copy.67
  1031.4 116.4 %all-to-all-done.1 = bf16[2,768,16,128]{3,1,0,2:T(8,128)(2,1)} async-done(((bf16[2,768,16,128]{3,1,0,2:T(8,128)(2,1)}), bf16[2,768,16,128]{3,1,0,2:T(8,128)(2,1)}, u32[]{:S(2)}, u32[]{:S(2)}) %all-to-all-start.1) | async-done | bytes 6291488 | tf_op jit(solution)/shard_map/all_to_all | solution.py:76
  1162.0 59.2 %copy.80 = bf16[2,6144,2,128]{3,2,1,0:T(2,128)(2,1)} copy(bf16[2,6144,2,128]{3,1,2,0:T(8,128)(2,1)S(1)} %bitcast.229) | data formatting | bytes 12582912
  1221.3 64.9 %all-to-all-done = bf16[2,768,16,128]{1,3,0,2:T(8,128)(2,1)} async-done(((bf16[2,768,16,128]{1,3,0,2:T(8,128)(2,1)}), bf16[2,768,16,128]{1,3,0,2:T(8,128)(2,1)}, u32[]{:S(2)}, u32[]{:S(2)}) %all-to-all-start) | async-done | bytes 6291488 | tf_op jit(solution)/shard_map/all_to_all | solution.py:75
  1286.2 12.8 reshape.195
  1298.9 15.5 fusion.140
  1314.5 14.1 copy.91
  1328.6 15.8 copy.90
  1356.2 498.0 %while.23 = (s32[]{:T(128)}, bf16[16,768,128]{1,2,0:T(8,128)(2,1)S(1)}, bf16[16,768,128]{1,2,0:T(8,128)(2,1)}, bf16[16,6144,128]{1,2,0:T(8,128)(2,1)}, bf16[16,6...) while((s32[]{:T(128)}, bf16[16,768,128]{1,2,0:T(8,128)(2,1)S(1)}, ...), condition=%wide.region_10.11_spmd.clone, body=%wide.region_7.10_spmd.clone.sunk | while | flops 2486794752 | bytes 61048408 | solution.py:37
  1866.2 33.1 %fusion.48 = f32[768,8192]{1,0:T(8,128)} fusion(bf16[2,2048,8192]{2,1,0:T(8,128)(2,1)} %param.23, bf16[768,2048]{1,0:T(8,128)(2,1)S(1)} %get-tuple-element.228, f32[2048]{0:T(1024)S(1)} %bitcast.247, f32[768]{0:T(1024)S(1)} %add_rsqrt_fusion), kind=kOutput, calls=%fused_computation.46 | convolution fusion | flops 25776095232 | bytes 61877248 | tf_op jit(solution)/shard_map/dot_general | solution.py:70
  1899.3 40.1 %multiply_convert_fusion.clone.5 = bf16[768,8192]{1,0:T(8,128)(2,1)} fusion(f32[768,8192]{1,0:T(8,128)} %fusion.48, bf16[2,2048,8192]{2,1,0:T(8,128)(2,1)} %param.24, bf16[768,2048]{1,0:T(8,128)(2,1)} %copy-done.29, f32[2048]{0:T(1024)S(1)} %bitcast.248, f32[768]{0:T(1024)S(1)} %add_rsqrt_fusion), kind=kOutput, calls=%fused_computation.60.clone.clone.clone.2 | convolution fusion | flops 25813843968 | bytes 74460160 | tf_op jit(solution)/shard_map/dot_general | solution.py:71
  1939.4 34.5 %fusion.93 = bf16[768,2048]{1,0:T(8,128)(2,1)} fusion(bf16[768,2048]{1,0:T(8,128)(2,1)S(1)} %copy-done.30, bf16[2,8192,2048]{2,1,0:T(8,128)(2,1)} %param.25, bf16[768,8192]{1,0:T(8,128)(2,1)} %multiply_convert_fusion.clone.5), kind=kOutput, calls=%fused_computation.105 | convolution fusion | flops 25774522368 | bytes 52428800 | tf_op jit(solution)/shard_map/dot_general | solution.py:72
  (278 shorter events, 1160.2 us)
Async XLA Ops:
  7.2 196.3 %all-gather.6.cloned.1.call-start = ((), (), s32[]{:S(2)}) async-start(), calls=%async_computation.2 | async-start | bytes 28311552 | tf_op jit(solution)/shard_map/all_gather | solution.py:65
  47.5 12.5 copy-start.15
  60.0 9.4 copy-start.12
  69.4 7.0 copy-start.21
  83.0 240.2 %all-gather.8.cloned.1.call-start = ((), (), s32[]{:S(2)}) async-start(), calls=%async_computation.3 | async-start | bytes 28311552 | tf_op jit(solution)/shard_map/all_gather | solution.py:66
  108.2 26.7 %copy-start.23 = (bf16[2,2048]{1,0:T(2,128)(2,1)S(1)}, bf16[2,2048]{1,0:T(2,128)(2,1)}, u32[]{:S(2)}) copy-start(bf16[2,2048]{1,0:T(2,128)(2,1)} %param.18) | copy-start | bytes 24580
  108.2 1247.6 %all-gather.12.cloned.1.call-start = ((), (), s32[]{:S(2)}) async-start(), calls=%async_computation.5 | async-start | bytes 28311552 | tf_op jit(solution)/shard_map/all_gather | solution.py:66
  325.2 508.3 %copy-start.16 = (bf16[768,2048]{1,0:T(8,128)(2,1)S(1)}, bf16[768,2048]{1,0:T(8,128)(2,1)}, u32[]{:S(2)}) copy-start(bf16[768,2048]{1,0:T(8,128)(2,1)} %param.15) | copy-start | bytes 9437188
  833.5 12.6 copy-start.26
  915.6 34.3 %copy-start.25 = (f32[1,2048]{1,0:T(1,128)S(1)}, f32[1,2048]{1,0:T(1,128)}, u32[]{:S(2)}) copy-start(f32[1,2048]{1,0:T(1,128)} %get-tuple-element.219) | copy-start | bytes 24580
  949.9 49.2 %copy-start.27 = (bf16[768,2048]{1,0:T(8,128)(2,1)}, bf16[768,2048]{1,0:T(8,128)(2,1)S(1)}, u32[]{:S(2)}) copy-start(bf16[768,2048]{1,0:T(8,128)(2,1)S(1)} %get-tuple-element.226) | copy-start | bytes 9437188
  964.6 391.2 %all-gather.10.cloned.1.call-start = ((), (), s32[]{:S(2)}) async-start(), calls=%async_computation.4 | async-start | bytes 28311552 | tf_op jit(solution)/shard_map/all_gather | solution.py:65
  989.3 9.7 copy-start.11
  999.0 7.1 copy-start.18
  999.0 7.1 copy-start.20
  1020.1 5.2 copy-start.1
  1020.1 5.3 copy-start.3
  1020.1 127.7 %all-to-all-start.1 = ((bf16[2,768,16,128]{3,1,0,2:T(8,128)(2,1)}), bf16[2,768,16,128]{3,1,0,2:T(8,128)(2,1)}, u32[]{:S(2)}, u32[]{:S(2)}) async-start(bf16[2,768,16,128]{3,1,0,2:T(8,128)(2,1)} %pad_maximum_fusion.1), calls=%async_computation.1 | async-start | bytes 12582912 | tf_op jit(solution)/shard_map/all_to_all | solution.py:76
  1031.4 121.7 %copy-start.13 = (bf16[768,16,64]{0,2,1:T(8,128)(2,1)S(1)}, bf16[768,16,64]{0,2,1:T(8,128)(2,1)}, u32[]{:S(2)}) copy-start(bf16[768,16,64]{0,2,1:T(8,128)(2,1)} %get-tuple-element.213) | copy-start | bytes 4718596
  1031.4 121.8 %copy-start.14 = (bf16[768,16,64]{0,2,1:T(8,128)(2,1)S(1)}, bf16[768,16,64]{0,2,1:T(8,128)(2,1)}, u32[]{:S(2)}) copy-start(bf16[768,16,64]{0,2,1:T(8,128)(2,1)} %get-tuple-element.214) | copy-start | bytes 4718596
  1147.8 138.3 %all-to-all-start = ((bf16[2,768,16,128]{1,3,0,2:T(8,128)(2,1)}), bf16[2,768,16,128]{1,3,0,2:T(8,128)(2,1)}, u32[]{:S(2)}, u32[]{:S(2)}) async-start(bf16[2,768,16,128]{1,3,0,2:T(8,128)(2,1)} %copy.72), calls=%async_computation | async-start | bytes 12582912 | tf_op jit(solution)/shard_map/all_to_all | solution.py:75
  1346.7 9.5 copy-start.22
  1854.1 12.1 copy-start.24
  1899.3 40.1 %copy-start.30 = (bf16[768,2048]{1,0:T(8,128)(2,1)S(1)}, bf16[768,2048]{1,0:T(8,128)(2,1)}, u32[]{:S(2)}) copy-start(bf16[768,2048]{1,0:T(8,128)(2,1)} %copy-done.29) | copy-start | bytes 9437188
  (13 other events, 24.5 us)
Sparse Core Ops, SparseCore 0:
  83.2 120.2 all-gather.5
  205.6 117.5 all-gather.7
  964.8 170.2 all-gather.11
  1136.5 191.3 all-gather.9
where the time goes:
time: 1990 us; the launch traced here: 1980 us
  matrix products  942 us (47%)
  other arithmetic  378 us (19%)
  waiting for transfers between devices  369 us (19%)
  local copies, waits for them, and re-layouts  240 us (12%)
  blocking collectives  24.7 us (1%)
    dot_general x32, matrix products, one(): jnp.einsum('qd,kd->qk', qh, kh, preferred_element_type=F32) * HEAD ** (-0.5)  345 us
    reduce_sum x32, other arithmetic, one(): p = jax.nn.softmax(jnp.where(mask, sc, -jnp.inf), axis=-1).astype(BF16)  344 us
    dot_general x32, matrix products, one(): return jnp.dot(p, vh, preferred_element_type=F32).astype(BF16)  300 us
    all_gather x2, waiting for transfers between devices, body(): vg = lax.all_gather(v, 'cp', tiled=True)  120 us
    all_to_all x1, waiting for transfers between devices, body(): vc = _natural(lax.all_to_all(jnp.stack(vl), 'cp', 2, 1, tiled=True), ncp)  116 us
    unnamed x68, local copies, waits for them, and re-layouts  101 us
    dot_general x2, matrix products, body(): jnp.dot(h2, w3[l], preferred_element_type=F32)  76.5 us
    dot_general x2, matrix products, body(): jnp.dot(u, w2[l], preferred_element_type=F32)  68.8 us
  transfers between devices with their start and end apart: 6, of which 4 were waited for; matrix products, arithmetic and copies ran while one was open for 11% of the time, Pallas kernels for 0%

commit v1 on v0

v1 whole, which is shorter than its diff:
```python
import functools

import jax
import jax.numpy as jnp
from jax import lax
from jax.experimental import pallas as pl
from jax.experimental.pallas import tpu as pltpu
from jax.sharding import PartitionSpec as P

HEAD = 128
F32 = jnp.float32
BF16 = jnp.bfloat16
LOG2E = 1.4426950408889634
MESH = pl.DeviceIdType.MESH
HBM = pl.BlockSpec(memory_space=pltpu.HBM)


class _Exchange:
    def __init__(self, ncp, srcs, dsts, scratch, first, second, last):
        self.ncp, self.srcs, self.dsts = ncp, srcs, dsts
        self.ssem, self.rsem, self.lsem, self.own = scratch
        self.first, self.second, self.last = first, second, last

    def _remote(self):
        me = lax.axis_index('cp')
        req = lax.axis_index('req')
        out = []
        for n, (s, d) in enumerate(zip(self.srcs, self.dsts)):
            for o in range(1, self.ncp):
                t = lax.rem(me + o, self.ncp)
                i = n * (self.ncp - 1) + o - 1
                out.append(pltpu.make_async_remote_copy(
                    s.at[t], d.at[me], self.ssem.at[i], self.rsem.at[i],
                    device_id=(req, t), device_id_type=MESH))
        return out

    def _load(self, n):
        return pltpu.make_async_copy(self.srcs[n].at[lax.axis_index('cp')], self.own.at[n], self.lsem.at[n])

    def _store(self, n):
        return pltpu.make_async_copy(self.own.at[n], self.dsts[n].at[lax.axis_index('cp')], self.lsem.at[n])

    def begin(self):
        if not self.srcs:
            return

        @pl.when(self.first)
        def _():
            me = lax.axis_index('cp')
            req = lax.axis_index('req')
            bar = pltpu.get_barrier_semaphore()
            for o in range(1, self.ncp):
                pl.semaphore_signal(bar, inc=1, device_id=(req, lax.rem(me + o, self.ncp)), device_id_type=MESH)
            pl.semaphore_wait(bar, self.ncp - 1)
            for c in self._remote():
                c.start()
            for n in range(len(self.srcs)):
                self._load(n).start()

    def end(self):
        if not self.srcs:
            return

        @pl.when(self.second)
        def _():
            for n in range(len(self.srcs)):
                self._load(n).wait()
                self._store(n).start()

        @pl.when(self.last)
        def _():
            for n in range(len(self.srcs)):
                self._store(n).wait()
            for c in self._remote():
                c.wait()


def _exchange_scratch(ncp, srcs):
    k = len(srcs)
    if not k:
        return []
    return [pltpu.SemaphoreType.DMA((k * (ncp - 1),)), pltpu.SemaphoreType.DMA((k * (ncp - 1),)),
            pltpu.SemaphoreType.DMA((k,)), pltpu.VMEM((k,) + srcs[0].shape[1:], BF16)]


class _Ids:
    def __init__(self):
        self.n = 0

    def params(self, comm):
        if not comm:
            return pltpu.CompilerParams(vmem_limit_bytes=62 << 20)
        self.n += 1
        return pltpu.CompilerParams(vmem_limit_bytes=62 << 20, collective_id=self.n, has_side_effects=True)


def _only_kernel(ncp, k, *refs):
    srcs, dsts, sc = refs[:k], refs[k:2 * k], refs[2 * k:]
    i = pl.program_id(0)
    ex = _Exchange(ncp, srcs, dsts, sc, i == 0, i == 0, i == 0)
    ex.begin()
    ex.end()


def _only(ids, ncp, srcs):
    k = len(srcs)
    return pl.pallas_call(
        functools.partial(_only_kernel, ncp, k), grid=(1,), in_specs=[HBM] * k, out_specs=[HBM] * k,
        out_shape=[jax.ShapeDtypeStruct(a.shape, a.dtype) for a in srcs],
        scratch_shapes=_exchange_scratch(ncp, srcs), compiler_params=ids.params(True), name='exchange')(*srcs)


def _attn_kernel(high, ncp, seg, big, k, *refs):
    nkv = 4 if high else 2
    q_ref, kv, srcs = refs[0], refs[1:1 + nkv], refs[1 + nkv:1 + nkv + k]
    o_ref, dsts = refs[1 + nkv + k], refs[2 + nkv + k:2 + nkv + 2 * k]
    sc = refs[2 + nkv + 2 * k:]
    m_s, acc, va = sc[0], sc[1], sc[2:2 + nkv // 2]
    b = pl.program_id(0)
    ex = _Exchange(ncp, srcs, dsts, sc[2 + nkv // 2:], b == 0, b == 1, b == ncp - 1) if k else None
    if k:
        ex.begin()
    kh, vh = kv[-2], va[-1]
    rows = kh.shape[0]
    nh = q_ref.shape[1] // HEAD
    scale = HEAD ** -0.5 * LOG2E

    @pl.when(b == 0)
    def _():
        for src, dst in zip(kv[1::2], va):
            for h in range(nh):
                dst[h, :, :HEAD] = src[:, h * HEAD:(h + 1) * HEAD]
                dst[h, :, HEAD:] = jnp.ones((rows, HEAD), BF16)

    m_s[...] = jnp.full_like(m_s, -jnp.inf)
    acc[...] = jnp.zeros_like(acc)

    def chunk(kr, vr, start, size, diag=None):
        start = pl.multiple_of(start, HEAD)
        ss = []
        for h in range(nh):
            hs = slice(h * HEAD, (h + 1) * HEAD)
            s = lax.dot_general(q_ref[:, hs], kr[pl.ds(start, size), hs], (((1,), (1,)), ((), ())),
                                preferred_element_type=F32)
            if diag is not None:
                c = lax.broadcasted_iota(jnp.int32, (seg, size), 1) - diag
                r = lax.broadcasted_iota(jnp.int32, (seg, size), 0)
                ok = c <= r
                if diag == 0 and size > seg:
                    ok = ok | (c >= seg)
                s = jnp.where(ok, s, -jnp.inf)
            ss.append(s)
        for h in range(nh):
            s = ss[h]
            mp = m_s[h]
            mn = jnp.maximum(mp, jnp.max(s, axis=1, keepdims=True))
            mc = mn * scale
            p = jnp.exp2(s * scale - mc[:, :1]).astype(BF16)
            al = jnp.exp2(mp * scale - mc)
            acc[h] = jnp.concatenate([al, al], axis=1) * acc[h] + jnp.dot(
                p, vr[h, pl.ds(start, size)], preferred_element_type=F32)
            m_s[h] = mn

    if high:
        for j in range(rows // big):
            chunk(kv[0], va[0], j * big, big)
    nb = (ncp - 1 - b) if high else b

    def pair(j, _):
        chunk(kh, vh, (rows - (j + 1) * 2 * seg) if high else j * 2 * seg, 2 * seg)
        return 0

    lax.fori_loop(0, nb // 2, pair, 0)

    @pl.when(lax.rem(nb, 2) == 1)
    def _():
        if high:
            chunk(kh, vh, b * seg, 2 * seg, 0)
        else:
            chunk(kh, vh, (b - 1) * seg, 2 * seg, seg)

    @pl.when(lax.rem(nb, 2) == 0)
    def _():
        chunk(kh, vh, b * seg, seg, 0)

    for h in range(nh):
        o_ref[:, h * HEAD:(h + 1) * HEAD] = (acc[h, :, :HEAD] / acc[h, :, HEAD:]).astype(BF16)
    if k:
        ex.end()


def _attention(ids, q, kv, send=()):
    ncp, seg, w = q.shape
    high, nh, k = len(kv) == 4, w // HEAD, len(send)
    rows = ncp * seg
    blk = pl.BlockSpec((None, seg, w), lambda i: (i, 0, 0))
    out = pl.pallas_call(
        functools.partial(_attn_kernel, high, ncp, seg, rows // 2, k),
        grid=(ncp,),
        in_specs=[blk] + [pl.BlockSpec((rows, w), lambda i: (0, 0))] * len(kv) + [HBM] * k,
        out_specs=[blk] + [HBM] * k,
        out_shape=[jax.ShapeDtypeStruct(q.shape, BF16)] + [jax.ShapeDtypeStruct(a.shape, BF16) for a in send],
        scratch_shapes=[pltpu.VMEM((nh, seg, HEAD), F32), pltpu.VMEM((nh, seg, 2 * HEAD), F32)]
        + [pltpu.VMEM((nh, rows, 2 * HEAD), BF16)] * (len(kv) // 2) + _exchange_scratch(ncp, send),
        compiler_params=ids.params(k), name='attn_high' if high else 'attn_low',
    )(q, *[a.reshape(rows, w) for a in kv], *send)
    return out[0], out[1:]


TN = 512


def _norm(x, g):
    x32 = x.astype(F32)
    r = lax.rsqrt(jnp.mean(x32 * x32, axis=-1, keepdims=True) + 1e-5)
    return (x32 * r * g.astype(F32)).astype(BF16)


def _dense_kernel(ncp, nm, nf, nq, cache, k, *refs):
    it = iter(refs)
    take = lambda n: [next(it) for _ in range(n)]
    x_ref, = take(1)
    if nm:
        o_ref, wo, g2, w1, w3, w2 = take(6)
    if nq:
        g1, cos, sin, wq, wk, wv = take(6)
    if cache:
        other, = take(1)
        land = take(8)
    srcs = take(k)
    if nm:
        y_ref, = take(1)
    if nq:
        qo, ko, vo = take(3)
    if cache:
        kc, vc = take(2)
    dsts = take(k)
    h_s, = take(1)
    if nm:
        o_s, x_s, acc = take(3)
    i = pl.program_id(0)
    last = nm + nf + 3 * nq - 1
    if k:
        ex = _Exchange(ncp, srcs, dsts, take(4), i == 0, i == 1, i == last)
        ex.begin()
    if nm:
        @pl.when(i == 0)
        def _():
            w = o_ref.shape[2]
            for j in range(ncp):
                o_s[:, j * w:(j + 1) * w] = o_ref[j]

        for j in range(nm):
            @pl.when(i == j)
            def _():
                ns = slice(j * TN, (j + 1) * TN)
                x_s[:, ns] = (x_ref[:, ns].astype(F32) + jnp.dot(
                    o_s[...], wo[...], preferred_element_type=F32)).astype(BF16)

        @pl.when(i == nm)
        def _():
            h_s[...] = _norm(x_s[...], g2[...])
            acc[...] = jnp.zeros_like(acc)

        @pl.when((i >= nm) & (i < nm + nf))
        def _():
            h = h_s[...]
            a = jnp.dot(h, w1[...], preferred_element_type=F32)
            c = jnp.dot(h, w3[...], preferred_element_type=F32)
            u = (jax.nn.silu(a) * c).astype(BF16)
            acc[...] += jnp.dot(u, w2[...], preferred_element_type=F32)

        @pl.when(i == nm + nf - 1)
        def _():
            y = (x_s[...].astype(F32) + acc[...]).astype(BF16)
            seg = x_s.shape[0]
            if cache:
                y_ref[:seg] = other[...]
                y_ref[seg:] = y
            else:
                y_ref[...] = y
            if nq:
                x_s[...] = y
    if nq:
        s = i - (nm + nf)

        @pl.when(s == 0)
        def _():
            h_s[...] = _norm(x_s[...] if nm else x_ref[...], g1[...])

        def project(w, out, rope):
            t = jnp.dot(h_s[...], w[...], preferred_element_type=F32)
            wd = out.shape[2]
            for j in range(TN // HEAD):
                th = t[:, j * HEAD:(j + 1) * HEAD]
                if rope:
                    th = th * cos[...] + pltpu.roll(th, HEAD // 2, 1) * sin[...]
                lo = j * HEAD % wd
                out[j * HEAD // wd, :, lo:lo + HEAD] = th.astype(BF16)

        @pl.when((s >= 0) & (s < nq))
        def _():
            project(wv, vo, False)

        @pl.when((s >= nq) & (s < 2 * nq))
        def _():
            project(wk, ko, True)

        @pl.when(s >= 2 * nq)
        def _():
            project(wq, qo, True)
    if cache:
        s = i - nm
        half = cache // 2

        def put(out, l, src):
            for h in range(out.shape[2]):
                out[l, :, h, :] = src[:, h * HEAD:(h + 1) * HEAD]

        @pl.when((s >= 0) & (s < half))
        def _():
            for l in range(2):
                put(kc, l, land[l])
                put(vc, l, land[4 + l])

        @pl.when((s >= half) & (s < cache))
        def _():
            for l in range(2):
                put(kc, l, land[2 + l])
                put(vc, l, land[6 + l])
    if k:
        ex.end()


def _dense(ids, ncp, x, half, mlp=None, qkv=None, cache=None, send=()):
    d = x.shape[1]
    seg = x.shape[0] // 2 if half is not None else x.shape[0]
    hb = half or 0
    k = len(send)
    nm = nf = nq = 0
    clamp = lambda v, n: jnp.clip(v, 0, n - 1)
    xs = pl.BlockSpec((seg, d), lambda i: (hb, 0))
    args, specs, outs, ospecs, scratch = [x], [xs], [], [], [pltpu.VMEM((seg, d), BF16)]
    if mlp is not None:
        l, o, wo, g2, w1, w3, w2 = mlp
        ff = w1.shape[2]
        nm, nf = d // TN, ff // TN
        nm_, nf_ = nm, nf
        args += [o, wo, g2, w1, w3, w2]
        specs += [pl.BlockSpec(o.shape, lambda i: (0, 0, 0)),
                  pl.BlockSpec((None, d, TN), lambda i: (l, 0, clamp(i, nm_))),
                  pl.BlockSpec((1, d), lambda i: (0, 0)),
                  pl.BlockSpec((None, d, TN), lambda i: (l, 0, clamp(i - nm_, nf_))),
                  pl.BlockSpec((None, d, TN), lambda i: (l, 0, clamp(i - nm_, nf_))),
                  pl.BlockSpec((None, TN, d), lambda i: (l, clamp(i - nm_, nf_), 0))]
        scratch += [pltpu.VMEM((seg, d), BF16), pltpu.VMEM((seg, d), BF16), pltpu.VMEM((seg, d), F32)]
    base = nm + nf
    if qkv is not None:
        lq, g1, cos, sin, wq, wk, wv = qkv
        nq = wq.shape[2] // TN
        nq_ = nq
        cs = pl.BlockSpec((seg, HEAD), lambda i: (qkv_half, 0))
        qkv_half = 0
        args += [g1, cos, sin, wq, wk, wv]
        specs += [pl.BlockSpec((1, d), lambda i: (0, 0)), cs, cs]
        specs += [pl.BlockSpec((None, d, TN), lambda i, p=p: (lq, 0, clamp(i - base - p * nq_, nq_))) for p in (2, 1, 0)]
    if cache is not None:
        other, land = cache
        w = land[0].shape[2]
        args += [other] + list(land)
        lo = pl.BlockSpec((None, seg, w), lambda i: (clamp(i - nm_, ncp), 0, 0))
        hi = pl.BlockSpec((None, seg, w), lambda i: (ncp - 1 - clamp(i - nm_ - ncp, ncp), 0, 0))
        specs += [pl.BlockSpec((seg, d), lambda i: (0, 0))] + [lo, lo, hi, hi] * 2
    args += list(send)
    specs += [HBM] * k
    if mlp is not None:
        ys = (2 * seg, d) if cache is not None else (seg, d)
        outs.append(jax.ShapeDtypeStruct(ys, BF16))
        ospecs.append(pl.BlockSpec(ys, lambda i: (0, 0)))
    if qkv is not None:
        wd = wq.shape[2] // ncp
        for p in (2, 1, 0):
            outs.append(jax.ShapeDtypeStruct((ncp, seg, wd), BF16))
            ospecs.append(pl.BlockSpec((TN // wd, seg, wd), lambda i, p=p: (clamp(i - base - p * nq_, nq_), 0, 0)))
    if cache is not None:
        for _ in range(2):
            outs.append(jax.ShapeDtypeStruct((2, 2 * ncp * seg, w // HEAD, HEAD), BF16))
            ospecs.append(pl.BlockSpec((2, seg, w // HEAD, HEAD), lambda i: (0, clamp(i - nm_, 2 * ncp), 0, 0)))
    outs += [jax.ShapeDtypeStruct(a.shape, BF16) for a in send]
    ospecs += [HBM] * k
    out = pl.pallas_call(
        functools.partial(_dense_kernel, ncp, nm, nf, nq, 2 * ncp if cache is not None else 0, k),
        grid=(nm + nf + 3 * nq,), in_specs=specs, out_specs=ospecs, out_shape=outs,
        scratch_shapes=scratch + _exchange_scratch(ncp, send), compiler_params=ids.params(k),
        name='dense' + ('_mlp' if nm else '') + ('_qkv' if nq else ''))(*args)
    return out[:len(out) - k], out[len(out) - k:]


def _angles(pos):
    half = HEAD // 2
    inv = 1.0 / (10000.0 ** (jnp.arange(half, dtype=F32) * (2.0 / HEAD)))
    ang = pos.astype(F32)[:, None] * inv
    c, s = jnp.cos(ang), jnp.sin(ang)
    return jnp.concatenate([c, c], axis=-1), jnp.concatenate([-s, s], axis=-1)


def solution(mesh):
    ncp = mesh.shape['cp']
    act = P(('req', 'cp'), None)
    cache = P(None, 'req', 'cp', None)

    def body(x, pos, g1, g2, wq, wk, wv, wo, w1, w3, w2):
        ids = _Ids()
        seg = x.shape[0] // 2
        cos, sin = _angles(pos)
        cl, sl, ch, sh = cos[:seg], sin[:seg], cos[seg:], sin[seg:]

        def qkv(l, c, s):
            return (l, g1[l:l + 1], c, s, wq, wk, wv)

        def mlp(l, o):
            return (l, o, wo, g2[l:l + 1], w1, w3, w2)

        dense = functools.partial(_dense, ids, ncp)
        a0l, _ = dense(x, 0, qkv=qkv(0, cl, sl))
        a0h, (q, k0l, v0l) = dense(x, 1, qkv=qkv(0, ch, sh), send=a0l)
        o, (v0h,) = _attention(ids, q, (k0l, v0l), send=(a0h[2],))
        (o,) = _only(ids, ncp, (o,))
        (xl, *a1l), (qh, k0h) = dense(x, 0, mlp=mlp(0, o), qkv=qkv(1, cl, sl), send=(a0h[0], a0h[1]))
        oh, (q, k1l, v1l) = _attention(ids, qh, (k0l, v0l, k0h, v0h), send=tuple(a1l))
        o, (oh,) = _attention(ids, q, (k1l, v1l), send=(oh,))
        (xh, *a1h), (o,) = dense(x, 1, mlp=mlp(0, oh), qkv=qkv(1, ch, sh), send=(o,))
        (xl,), (q, k1h, v1h) = dense(xl, None, mlp=mlp(1, o), send=tuple(a1h))
        o, _ = _attention(ids, q, (k1l, v1l, k1h, v1h))
        (o,) = _only(ids, ncp, (o,))
        (y, kc, vc), _ = dense(xh, None, mlp=mlp(1, o), cache=(xl, (k0l, k1l, k0h, k1h, v0l, v1l, v0h, v1h)))
        return y, kc, vc

    return jax.shard_map(body, mesh=mesh, in_specs=(act, P(('req', 'cp'))) + (P(),) * 9,
                         out_specs=(act, cache, cache), check_vma=False)
```

time: 1990 us -> 648 us (0.33)
  matrix products: 942 us -> 0 us
  Pallas kernels: 0 us -> 629 us
  other arithmetic: 378 us -> 3.31 us
  waiting for transfers between devices: 369 us -> 0 us
  local copies, waits for them, and re-layouts: 240 us -> 1.41 us
  blocking collectives: 24.7 us -> 0 us
    dot_general x78 -> x0, matrix products: 942 us -> none  [the longest x32 345 us: one(): jnp.einsum('qd,kd->qk', qh, kh, preferred_element_type=F32) * HEAD ** (-0.5)]
    pallas_call x0 -> x12, Pallas kernels: none -> 629 us  [the longest x6 409 us: _dense(): pl.pallas_call(functools.partial(_dense_kernel, ncp, nm, nf, nq, 2 * ncp...]
    reduce_sum x33 -> x0, other arithmetic: 347 us -> none  [the longest x32 344 us: one(): p = jax.nn.softmax(jnp.where(mask, sc, -jnp.inf), axis=-1).astype(BF16)]
    all_gather x4 -> x0, waiting for transfers between devices: 188 us -> none  [the longest x2 120 us: body(): vg = lax.all_gather(v, 'cp', tiled=True)]
    all_to_all x2 -> x0, waiting for transfers between devices: 181 us -> none  [the longest x1 116 us: body(): vc = _natural(lax.all_to_all(jnp.stack(vl), 'cp', 2, 1, tiled=True), ncp)]
    unnamed x68 -> x0, local copies, waits for them, and re-layouts: 101 us -> none
    dot_general x6 -> x0, local copies, waits for them, and re-layouts: 73.4 us -> none  [the longest x3 36.7 us: body(): jnp.dot(h, wq[l], preferred_element_type=F32).reshape(s_dev, nh, HEAD)]
    all_gather x1 -> x0, blocking collectives: 24.7 us -> none  [body(): pos_all = lax.all_gather(pos, 'cp', tiled=True)]
  transfers between devices with their start and end apart: 6 -> 0, of which waited for: 4 -> 0; matrix products, arithmetic and copies ran while one was open for 11% -> 0% of each run, Pallas kernels for 0% -> 0%
where the time goes in v1:
time: 648 us; the launch traced here: 635 us
  Pallas kernels  629 us (97%)
    pallas_call x6, Pallas kernels, _dense(): pl.pallas_call(functools.partial(_dense_kernel, ncp, nm, nf, nq, 2 * ncp...  409 us
    pallas_call x4, Pallas kernels, _attention(): pl.pallas_call(functools.partial(_attn_kernel, high, ncp, seg, rows // 2,...  181 us
    pallas_call x2, Pallas kernels, _only(): pl.pallas_call(functools.partial(_only_kernel, ncp, k), grid=(1,), in_spe...  40 us

profile of v1, /device:TPU:112, one launch (start us, length us, event | category | flops | bytes accessed | tf_op | source)
XLA Modules:
  0.0 635.4 jit_solution(15682306911933042035)
XLA Ops:
  0.6 0.7 convert_element_type.3
  1.3 1.4 fusion.3
  2.7 1.4 multiply_sine_fusion
  4.2 1.2 pad_maximum_fusion
  5.4 21.4 %dense_qkv.2 = (bf16[8,384,256]{2,1,0:T(8,128)(2,1)}, bf16[8,384,256]{2,1,0:T(8,128)(2,1)}, bf16[8,384,256]{2,1,0:T(8,128)(2,1)}) custom-call(bf16[768,2048]{1,0:T(8,128)(2,1)} %refs_0_.7, bf16[1,2048]{1,0:T(2,128)(2,1)} %get-tuple-element.80.refs_1_, f32[384,128]{1,0:T(8,128)} %get-tuple-element.79.refs_2_.refs_8_, ...), custom_call_target="tpu_custom_call" | custom-call | tf_op jit(solution)/shard_map/dense_qkv/pallas_call | solution.py:391
  26.8 60.2 %dense_qkv.3 = (bf16[8,384,256]{2,1,0:T(8,128)(2,1)}, bf16[8,384,256]{2,1,0:T(8,128)(2,1)}, bf16[8,384,256]{2,1,0:T(8,128)(2,1)}, bf16[8,384,256]{2,1,0:T(8,128)...) custom-call(bf16[768,2048]{1,0:T(8,128)(2,1)} %refs_0_.7, bf16[1,2048]{1,0:T(2,128)(2,1)} %get-tuple-element.80.refs_1_, ...), custom_call_target="tpu_custom_call" | custom-call | tf_op jit(solution)/shard_map/dense_qkv/pallas_call | solution.py:391
  87.0 32.4 %attn_low.2 = (bf16[8,384,256]{2,1,0:T(8,128)(2,1)}, bf16[8,384,256]{2,1,0:T(8,128)(2,1)}) custom-call(bf16[8,384,256]{2,1,0:T(8,128)(2,1)} %get-tuple-element.38.refs_0_, bf16[3072,256]{1,0:T(8,128)(2,1)} %bitcast.8, bf16[3072,256]{1,0:T(8,128)(2,1)} %bitcast.10, bf16[8,384,256]{2,1,0:T(8,128)(2,1)} %get-tuple-element.41.refs_3_), custom_call_target="tpu_custom_call" | custom-call | tf_op jit(solution)/shard_map/attn_low/pallas_call | solution.py:197
  119.4 19.2 %exchange.2.refs_1_ = bf16[8,384,256]{2,1,0:T(8,128)(2,1)} custom-call(bf16[8,384,256]{2,1,0:T(8,128)(2,1)} %get-tuple-element.42.refs_0_), custom_call_target="tpu_custom_call" | custom-call | tf_op jit(solution)/shard_map/exchange/pallas_call | solution.py:107
  138.6 83.3 %dense_mlp_qkv.2 = (bf16[384,2048]{1,0:T(8,128)(2,1)}, bf16[8,384,256]{2,1,0:T(8,128)(2,1)}, bf16[8,384,256]{2,1,0:T(8,128)(2,1)}, bf16[8,384,256]{2,1,0:T(8,128...) custom-call(bf16[768,2048]{1,0:T(8,128)(2,1)} %refs_0_.7, bf16[8,384,256]{2,1,0:T(8,128)(2,1)} %exchange.2.refs_1_, ...), custom_call_target="tpu_custom_call" | custom-call | tf_op jit(solution)/shard_map/dense_mlp_qkv/pallas_call | solution.py:391
  221.9 60.6 %attn_high.2 = (bf16[8,384,256]{2,1,0:T(8,128)(2,1)}, bf16[8,384,256]{2,1,0:T(8,128)(2,1)}, bf16[8,384,256]{2,1,0:T(8,128)(2,1)}, bf16[8,384,256]{2,1,0:T(8,128)(2,1)}) custom-call(bf16[8,384,256]{2,1,0:T(8,128)(2,1)} %get-tuple-element.45.refs_0_, bf16[3072,256]{1,0:T(8,128)(2,1)} %bitcast.9, bf16[3072,256]{1,0:T(8,128)(2,1)} %bitcast.11, ...), custom_call_target="tpu_custom_call" | custom-call | tf_op jit(solution)/shard_map/attn_high/pallas_call | solution.py:197
  282.6 30.3 %attn_low.3 = (bf16[8,384,256]{2,1,0:T(8,128)(2,1)}, bf16[8,384,256]{2,1,0:T(8,128)(2,1)}) custom-call(bf16[8,384,256]{2,1,0:T(8,128)(2,1)} %get-tuple-element.51.refs_0_, bf16[3072,256]{1,0:T(8,128)(2,1)} %bitcast.12, bf16[3072,256]{1,0:T(8,128)(2,1)} %bitcast.14, bf16[8,384,256]{2,1,0:T(8,128)(2,1)} %get-tuple-element.54.refs_3_), custom_call_target="tpu_custom_call" | custom-call | tf_op jit(solution)/shard_map/attn_low/pallas_call | solution.py:197
  312.9 81.2 %dense_mlp_qkv.3 = (bf16[384,2048]{1,0:T(8,128)(2,1)}, bf16[8,384,256]{2,1,0:T(8,128)(2,1)}, bf16[8,384,256]{2,1,0:T(8,128)(2,1)}, bf16[8,384,256]{2,1,0:T(8,128)(2,1)}, bf16[8,384,256]{2,1,0:T(8,128)(2,1)}) custom-call(bf16[768,2048]{1,0:T(8,128)(2,1)} %refs_0_.7, bf16[8,384,256]{2,1,0:T(8,128)(2,1)} %get-tuple-element.55.refs_1_, ...), custom_call_target="tpu_custom_call" | custom-call | tf_op jit(solution)/shard_map/dense_mlp_qkv/pallas_call | solution.py:391
  394.1 59.0 %dense_mlp.2 = (bf16[384,2048]{1,0:T(8,128)(2,1)}, bf16[8,384,256]{2,1,0:T(8,128)(2,1)}, bf16[8,384,256]{2,1,0:T(8,128)(2,1)}, bf16[8,384,256]{2,1,0:T(8,128)(2,1)}) custom-call(bf16[384,2048]{1,0:T(8,128)(2,1)} %get-tuple-element.58.refs_0_, bf16[8,384,256]{2,1,0:T(8,128)(2,1)} %get-tuple-element.59.refs_1_, bf16[2,2048,2048]{2,1,0:T(8,128)(2,1)} %refs_2_.7, ...), custom_call_target="tpu_custom_call" | custom-call | tf_op jit(solution)/shard_map/dense_mlp/pallas_call | solution.py:391
  453.1 57.2 %attn_high.3.refs_0_ = bf16[8,384,256]{2,1,0:T(8,128)(2,1)} custom-call(bf16[8,384,256]{2,1,0:T(8,128)(2,1)} %get-tuple-element.63.refs_0_, bf16[3072,256]{1,0:T(8,128)(2,1)} %bitcast.13, bf16[3072,256]{1,0:T(8,128)(2,1)} %bitcast.15, bf16[3072,256]{1,0:T(8,128)(2,1)} %bitcast.18, bf16[3072,256]{1,0:T(8,128)(2,1)} %bitcast.19), custom_call_target="tpu_custom_call" | custom-call | tf_op jit(solution)/shard_map/attn_high/pallas_call | solution.py:197
  510.3 20.8 %exchange.3.refs_1_ = bf16[8,384,256]{2,1,0:T(8,128)(2,1)} custom-call(bf16[8,384,256]{2,1,0:T(8,128)(2,1)} %attn_high.3.refs_0_), custom_call_target="tpu_custom_call" | custom-call | tf_op jit(solution)/shard_map/exchange/pallas_call | solution.py:107
  531.1 103.8 %dense_mlp.3 = (bf16[768,2048]{1,0:T(8,128)(2,1)}, bf16[2,6144,2,128]{3,2,1,0:T(2,128)(2,1)}, bf16[2,6144,2,128]{3,2,1,0:T(2,128)(2,1)}) custom-call(bf16[384,2048]{1,0:T(8,128)(2,1)} %get-tuple-element.57.refs_0_, bf16[8,384,256]{2,1,0:T(8,128)(2,1)} %exchange.3.refs_1_, bf16[2,2048,2048]{2,1,0:T(8,128)(2,1)} %refs_2_.7, ...), custom_call_target="tpu_custom_call" | custom-call | tf_op jit(solution)/shard_map/dense_mlp/pallas_call | solution.py:391
  (1 shorter events, 0.0 us)

commit v2 on v1

--- a/solution.py
+++ b/solution.py
@@ -40,27 +40,17 @@
     def _store(self, n):
         return pltpu.make_async_copy(self.own.at[n], self.dsts[n].at[lax.axis_index('cp')], self.lsem.at[n])
 
-    def begin(self):
-        if not self.srcs:
-            return
-
+    def begin(self, greet=True):
         @pl.when(self.first)
         def _():
-            me = lax.axis_index('cp')
-            req = lax.axis_index('req')
-            bar = pltpu.get_barrier_semaphore()
-            for o in range(1, self.ncp):
-                pl.semaphore_signal(bar, inc=1, device_id=(req, lax.rem(me + o, self.ncp)), device_id_type=MESH)
-            pl.semaphore_wait(bar, self.ncp - 1)
+            if greet:
+                _greet(self.ncp)
             for c in self._remote():
                 c.start()
             for n in range(len(self.srcs)):
                 self._load(n).start()
 
     def end(self):
-        if not self.srcs:
-            return
-
         @pl.when(self.second)
         def _():
             for n in range(len(self.srcs)):
@@ -94,97 +84,146 @@
         return pltpu.CompilerParams(vmem_limit_bytes=62 << 20, collective_id=self.n, has_side_effects=True)
 
 
-def _only_kernel(ncp, k, *refs):
-    srcs, dsts, sc = refs[:k], refs[k:2 * k], refs[2 * k:]
-    i = pl.program_id(0)
-    ex = _Exchange(ncp, srcs, dsts, sc, i == 0, i == 0, i == 0)
-    ex.begin()
-    ex.end()
-
-
-def _only(ids, ncp, srcs):
-    k = len(srcs)
-    return pl.pallas_call(
-        functools.partial(_only_kernel, ncp, k), grid=(1,), in_specs=[HBM] * k, out_specs=[HBM] * k,
-        out_shape=[jax.ShapeDtypeStruct(a.shape, a.dtype) for a in srcs],
-        scratch_shapes=_exchange_scratch(ncp, srcs), compiler_params=ids.params(True), name='exchange')(*srcs)
-
-
-def _attn_kernel(high, ncp, seg, big, k, *refs):
+def _greet(ncp):
+    me = lax.axis_index('cp')
+    req = lax.axis_index('req')
+    bar = pltpu.get_barrier_semaphore()
+    for o in range(1, ncp):
+        pl.semaphore_signal(bar, inc=1, device_id=(req, lax.rem(me + o, ncp)), device_id_type=MESH)
+    pl.semaphore_wait(bar, ncp - 1)
+
+
+EXTRA = 16
+
+
+def _attn_kernel(high, ncp, k, *refs):
     nkv = 4 if high else 2
     q_ref, kv, srcs = refs[0], refs[1:1 + nkv], refs[1 + nkv:1 + nkv + k]
-    o_ref, dsts = refs[1 + nkv + k], refs[2 + nkv + k:2 + nkv + 2 * k]
+    land, dsts = refs[1 + nkv + k], refs[2 + nkv + k:2 + nkv + 2 * k]
     sc = refs[2 + nkv + 2 * k:]
-    m_s, acc, va = sc[0], sc[1], sc[2:2 + nkv // 2]
-    b = pl.program_id(0)
-    ex = _Exchange(ncp, srcs, dsts, sc[2 + nkv // 2:], b == 0, b == 1, b == ncp - 1) if k else None
+    s_s, m_s, acc, out, ssem, rsem, lsem = sc[:7]
+    vt = sc[7:7 + nkv // 2]
+    i = pl.program_id(0)
+    rows, w = q_ref.shape
+    seg = rows // ncp
+    c2 = 2 * seg
+    npair = ncp // 2
+    nh = w // HEAD
+    scale = HEAD ** -0.5 * LOG2E
+    me = lax.axis_index('cp')
+    req = lax.axis_index('req')
+    b = lax.rem(me // 2 + 1 + i, npair)
+    ex = _Exchange(ncp, srcs, dsts, sc[7 + nkv // 2:], i == 0, i == 1, i == npair - 1) if k else None
+
+    @pl.when(i == 0)
+    def _():
+        _greet(ncp)
+
     if k:
-        ex.begin()
-    kh, vh = kv[-2], va[-1]
-    rows = kh.shape[0]
-    nh = q_ref.shape[1] // HEAD
-    scale = HEAD ** -0.5 * LOG2E
-
-    @pl.when(b == 0)
-    def _():
-        for src, dst in zip(kv[1::2], va):
+        ex.begin(greet=False)
+
+    @pl.when(i == 0)
+    def _():
+        for src, dst in zip(kv[1::2], vt):
             for h in range(nh):
-                dst[h, :, :HEAD] = src[:, h * HEAD:(h + 1) * HEAD]
-                dst[h, :, HEAD:] = jnp.ones((rows, HEAD), BF16)
+                for j in range(npair):
+                    dst[h, :HEAD, j * c2:(j + 1) * c2] = src[j * c2:(j + 1) * c2, h * HEAD:(h + 1) * HEAD].T
+                dst[h, HEAD:, :] = jnp.ones((EXTRA, rows), BF16)
 
     m_s[...] = jnp.full_like(m_s, -jnp.inf)
     acc[...] = jnp.zeros_like(acc)
 
-    def chunk(kr, vr, start, size, diag=None):
-        start = pl.multiple_of(start, HEAD)
-        ss = []
+    def scores(kr, start, h):
+        hs = slice(h * HEAD, (h + 1) * HEAD)
+        s_s[h] = lax.dot_general(kr[pl.ds(pl.multiple_of(start, c2), c2), hs], q_ref[pl.ds(pl.multiple_of(b * c2, c2), c2), hs],
+                                 (((1,), (1,)), ((), ())), preferred_element_type=F32)
+
+    def update(vr, start, h, mask=False):
+        s = s_s[h]
+        if mask:
+            r = lax.broadcasted_iota(jnp.int32, (c2, c2), 0)
+            c = lax.broadcasted_iota(jnp.int32, (c2, c2), 1)
+            if high:
+                r = jnp.where(r >= seg, r - seg, r + seg)
+                c = jnp.where(c >= seg, c - seg, c + seg)
+            s = jnp.where(r <= c, s, -jnp.inf)
+        mp = m_s[h]
+        mn = jnp.maximum(mp, jnp.max(s, axis=0, keepdims=True))
+        mc = mn * scale
+        p = jnp.exp2(s * scale - mc).astype(BF16)
+        al = jnp.exp2(mp * scale - mc)
+        acc[h] = acc[h] * al + jnp.dot(vr[h, :, pl.ds(pl.multiple_of(start, c2), c2)], p, preferred_element_type=F32)
+        m_s[h] = mn
+
+    def chunk(kr, vr, start, nkr, nstart):
         for h in range(nh):
-            hs = slice(h * HEAD, (h + 1) * HEAD)
-            s = lax.dot_general(q_ref[:, hs], kr[pl.ds(start, size), hs], (((1,), (1,)), ((), ())),
-                                preferred_element_type=F32)
-            if diag is not None:
-                c = lax.broadcasted_iota(jnp.int32, (seg, size), 1) - diag
-                r = lax.broadcasted_iota(jnp.int32, (seg, size), 0)
-                ok = c <= r
-                if diag == 0 and size > seg:
-                    ok = ok | (c >= seg)
-                s = jnp.where(ok, s, -jnp.inf)
-            ss.append(s)
-        for h in range(nh):
-            s = ss[h]
-            mp = m_s[h]
-            mn = jnp.maximum(mp, jnp.max(s, axis=1, keepdims=True))
-            mc = mn * scale
-            p = jnp.exp2(s * scale - mc[:, :1]).astype(BF16)
-            al = jnp.exp2(mp * scale - mc)
-            acc[h] = jnp.concatenate([al, al], axis=1) * acc[h] + jnp.dot(
-                p, vr[h, pl.ds(start, size)], preferred_element_type=F32)
-            m_s[h] = mn
+            if h + 1 < nh:
+                scores(kr, start, h + 1)
+            else:
+                scores(nkr, nstart, 0)
+            update(vr, start, h)
+
+    kh, vh = kv[-2], vt[-1]
+    nb = (npair - 1 - b) if high else b
+
+    def at(j):
+        return (npair - 1 - j) * c2 if high else j * c2
 
     if high:
-        for j in range(rows // big):
-            chunk(kv[0], va[0], j * big, big)
-    nb = (ncp - 1 - b) if high else b
-
-    def pair(j, _):
-        chunk(kh, vh, (rows - (j + 1) * 2 * seg) if high else j * 2 * seg, 2 * seg)
+        scores(kv[0], 0, 0)
+        for j in range(npair):
+            if j + 1 < npair:
+                chunk(kv[0], vt[0], j * c2, kv[0], (j + 1) * c2)
+            else:
+                chunk(kv[0], vt[0], j * c2, kh, at(0))
+    else:
+        scores(kh, 0, 0)
+
+    def body(j, _):
+        chunk(kh, vh, at(j), kh, at(j + 1))
         return 0
 
-    lax.fori_loop(0, nb // 2, pair, 0)
-
-    @pl.when(lax.rem(nb, 2) == 1)
-    def _():
-        if high:
-            chunk(kh, vh, b * seg, 2 * seg, 0)
-        else:
-            chunk(kh, vh, (b - 1) * seg, 2 * seg, seg)
-
-    @pl.when(lax.rem(nb, 2) == 0)
-    def _():
-        chunk(kh, vh, b * seg, seg, 0)
-
+    lax.fori_loop(0, nb, body, 0)
     for h in range(nh):
-        o_ref[:, h * HEAD:(h + 1) * HEAD] = (acc[h, :, :HEAD] / acc[h, :, HEAD:]).astype(BF16)
+        if h + 1 < nh:
+            scores(kh, b * c2, h + 1)
+        update(vh, b * c2, h, True)
+    for h in range(nh):
+        o = acc[h, :HEAD] / acc[h, HEAD:HEAD + 1]
+        out[i, :, h * HEAD:(h + 1) * HEAD] = o.T.astype(BF16)
+
+    def send(step, pair, e):
+        return pltpu.make_async_remote_copy(
+            out.at[step, pl.ds(e * seg, seg)], land.at[me], ssem.at[2 * step + e], rsem.at[2 * step + lax.rem(me, 2)],
+            device_id=(req, 2 * pair + e), device_id_type=MESH)
+
+    @pl.when(i < npair - 1)
+    def _():
+        for e in range(2):
+            send(i, b, e).start()
+
+    @pl.when(i == npair - 1)
+    def _():
+        mine = lax.rem(me, 2)
+        peer = 1 - mine
+        last = npair - 1
+        own = pltpu.make_async_copy(out.at[last, pl.ds(mine * seg, seg)], land.at[me], lsem)
+        own.start()
+        twin = pltpu.make_async_remote_copy(
+            out.at[last, pl.ds(peer * seg, seg)], land.at[me], ssem.at[2 * last], rsem.at[2 * last],
+            device_id=(req, me + 1 - 2 * mine), device_id_type=MESH)
+        twin.start()
+        for step in range(last):
+            pair = lax.rem(me // 2 + 1 + step, npair)
+            for e in range(2):
+                send(step, pair, e).wait_send()
+                src = 2 * lax.rem(me // 2 + npair - 1 - step, npair) + e
+                pltpu.make_async_remote_copy(
+                    out.at[step, pl.ds(e * seg, seg)], land.at[src], ssem.at[2 * step + e], rsem.at[2 * step + e],
+                    device_id=(req, src), device_id_type=MESH).wait_recv()
+        twin.wait()
+        own.wait()
+
     if k:
         ex.end()
 
@@ -192,19 +231,105 @@
 def _attention(ids, q, kv, send=()):
     ncp, seg, w = q.shape
     high, nh, k = len(kv) == 4, w // HEAD, len(send)
-    rows = ncp * seg
-    blk = pl.BlockSpec((None, seg, w), lambda i: (i, 0, 0))
+    rows, c2, npair = ncp * seg, 2 * seg, ncp // 2
+    flat = pl.BlockSpec((rows, w), lambda i: (0, 0))
     out = pl.pallas_call(
-        functools.partial(_attn_kernel, high, ncp, seg, rows // 2, k),
-        grid=(ncp,),
-        in_specs=[blk] + [pl.BlockSpec((rows, w), lambda i: (0, 0))] * len(kv) + [HBM] * k,
-        out_specs=[blk] + [HBM] * k,
-        out_shape=[jax.ShapeDtypeStruct(q.shape, BF16)] + [jax.ShapeDtypeStruct(a.shape, BF16) for a in send],
-        scratch_shapes=[pltpu.VMEM((nh, seg, HEAD), F32), pltpu.VMEM((nh, seg, 2 * HEAD), F32)]
-        + [pltpu.VMEM((nh, rows, 2 * HEAD), BF16)] * (len(kv) // 2) + _exchange_scratch(ncp, send),
-        compiler_params=ids.params(k), name='attn_high' if high else 'attn_low',
-    )(q, *[a.reshape(rows, w) for a in kv], *send)
+        functools.partial(_attn_kernel, high, ncp, k),
+        grid=(npair,),
+        in_specs=[flat] * (1 + len(kv)) + [HBM] * k,
+        out_specs=[HBM] * (1 + k),
+        out_shape=[jax.ShapeDtypeStruct(a.shape, BF16) for a in (q,) + tuple(send)],
+        scratch_shapes=[pltpu.VMEM((nh, c2, c2), F32), pltpu.VMEM((nh, 1, c2), F32), pltpu.VMEM((nh, HEAD + EXTRA, c2), F32),
+                        pltpu.VMEM((npair, c2, w), BF16), pltpu.SemaphoreType.DMA((ncp,)), pltpu.SemaphoreType.DMA((ncp,)),
+                        pltpu.SemaphoreType.DMA]
+        + [pltpu.VMEM((nh, HEAD + EXTRA, rows), BF16)] * (len(kv) // 2) + _exchange_scratch(ncp, send),
+        compiler_params=ids.params(True), name='attn_high' if high else 'attn_low',
+    )(q.reshape(rows, w), *[a.reshape(rows, w) for a in kv], *send)
     return out[0], out[1:]
+
+
+def _first_kernel(ncp, nq, x_ref, g1, cos, sin, wq, wk, wv, qh, kh, vh, ql, kl, vl, h_s, buf, ssem, rsem, lsem):
+    i = pl.program_id(0)
+    me = lax.axis_index('cp')
+    req = lax.axis_index('req')
+    seg = x_ref.shape[0] // 2
+    wd = qh.shape[2]
+    per = TN // wd
+
+    @pl.when(i == 0)
+    def _():
+        _greet(ncp)
+        h_s[...] = _norm(x_ref[...], g1[0:1])
+
+    def remote(p, t, dst):
+        return pltpu.make_async_remote_copy(buf.at[p, t], dst.at[me], ssem.at[p * ncp + t], rsem.at[p * ncp + me],
+                                            device_id=(req, t), device_id_type=MESH)
+
+    def own(p, dst):
+        return pltpu.make_async_copy(buf.at[p, me], dst.at[me], lsem.at[p])
+
+    def project(p, w, high, low, rope):
+        n = i - p * nq
+        t = jnp.dot(h_s[...], w[...], preferred_element_type=F32)
+        for j in range(TN // HEAD):
+            th = t[:, j * HEAD:(j + 1) * HEAD]
+            if rope:
+                th = th * cos[...] + pltpu.roll(th, HEAD // 2, 1) * sin[...]
+            th = th.astype(BF16)
+            lo = j * HEAD % wd
+            e = j * HEAD // wd
+            buf[p, per * n + e, :, lo:lo + HEAD] = th[:seg]
+            high[e, :, lo:lo + HEAD] = th[seg:]
+        for e in range(per):
+            to = per * n + e
+
+            @pl.when(to != me)
+            def _():
+                remote(p, to, low).start()
+
+            @pl.when(to == me)
+            def _():
+                own(p, low).start()
+
+    @pl.when(i < nq)
+    def _():
+        project(0, wv, vh, vl, False)
+
+    @pl.when((i >= nq) & (i < 2 * nq))
+    def _():
+        project(1, wk, kh, kl, True)
+
+    @pl.when(i >= 2 * nq)
+    def _():
+        project(2, wq, qh, ql, True)
+
+    @pl.when(i == 3 * nq - 1)
+    def _():
+        for p, dst in enumerate((vl, kl, ql)):
+            own(p, dst).wait()
+            for o in range(1, ncp):
+                t = lax.rem(me + o, ncp)
+                remote(p, t, dst).wait_send()
+                pltpu.make_async_remote_copy(buf.at[p, t], dst.at[t], ssem.at[p * ncp + t], rsem.at[p * ncp + t],
+                                             device_id=(req, t), device_id_type=MESH).wait_recv()
+
+
+def _first(ids, ncp, x, g1, cos, sin, wq, wk, wv):
+    rows, d = x.shape
+    seg, wd, nq = rows // 2, wq.shape[2] // ncp, wq.shape[2] // TN
+    clamp = lambda v, n: jnp.clip(v, 0, n - 1)
+    full = lambda a: pl.BlockSpec(a.shape, lambda i: (0, 0))
+    blocks = jax.ShapeDtypeStruct((ncp, seg, wd), BF16)
+    out = pl.pallas_call(
+        functools.partial(_first_kernel, ncp, nq), grid=(3 * nq,),
+        in_specs=[full(x), full(g1), full(cos), full(sin)]
+        + [pl.BlockSpec((None, d, TN), lambda i, p=p: (0, 0, clamp(i - p * nq, nq))) for p in (2, 1, 0)],
+        out_specs=[pl.BlockSpec((TN // wd, seg, wd), lambda i, p=p: (clamp(i - p * nq, nq), 0, 0)) for p in (2, 1, 0)] + [HBM] * 3,
+        out_shape=[blocks] * 6,
+        scratch_shapes=[pltpu.VMEM((rows, d), BF16), pltpu.VMEM((3, ncp, seg, wd), BF16), pltpu.SemaphoreType.DMA((3 * ncp,)),
+                        pltpu.SemaphoreType.DMA((3 * ncp,)), pltpu.SemaphoreType.DMA((3,))],
+        compiler_params=ids.params(True), name='first_qkv')(x, g1, cos, sin, wq, wk, wv)
+    return out[:3], out[3:]
 
 
 TN = 512
@@ -216,7 +341,7 @@
     return (x32 * r * g.astype(F32)).astype(BF16)
 
 
-def _dense_kernel(ncp, nm, nf, nq, cache, k, *refs):
+def _dense_kernel(ncp, nm, nf, nq, lm, lq, cache, k, *refs):
     it = iter(refs)
     take = lambda n: [next(it) for _ in range(n)]
     x_ref, = take(1)
@@ -259,7 +384,7 @@
 
         @pl.when(i == nm)
         def _():
-            h_s[...] = _norm(x_s[...], g2[...])
+            h_s[...] = _norm(x_s[...], g2[lm:lm + 1])
             acc[...] = jnp.zeros_like(acc)
 
         @pl.when((i >= nm) & (i < nm + nf))
@@ -286,7 +411,7 @@
 
         @pl.when(s == 0)
         def _():
-            h_s[...] = _norm(x_s[...] if nm else x_ref[...], g1[...])
+            h_s[...] = _norm(x_s[...], g1[lq:lq + 1])
 
         def project(w, out, rope):
             t = jnp.dot(h_s[...], w[...], preferred_element_type=F32)
@@ -314,8 +439,7 @@
         half = cache // 2
 
         def put(out, l, src):
-            for h in range(out.shape[2]):
-                out[l, :, h, :] = src[:, h * HEAD:(h + 1) * HEAD]
+            out[l] = src[...].reshape(out.shape[1:])
 
         @pl.when((s >= 0) & (s < half))
         def _():
@@ -337,7 +461,7 @@
     seg = x.shape[0] // 2 if half is not None else x.shape[0]
     hb = half or 0
     k = len(send)
-    nm = nf = nq = 0
+    nm = nf = nq = l = lq = 0
     clamp = lambda v, n: jnp.clip(v, 0, n - 1)
     xs = pl.BlockSpec((seg, d), lambda i: (hb, 0))
     args, specs, outs, ospecs, scratch = [x], [xs], [], [], [pltpu.VMEM((seg, d), BF16)]
@@ -349,7 +473,7 @@
         args += [o, wo, g2, w1, w3, w2]
         specs += [pl.BlockSpec(o.shape, lambda i: (0, 0, 0)),
                   pl.BlockSpec((None, d, TN), lambda i: (l, 0, clamp(i, nm_))),
-                  pl.BlockSpec((1, d), lambda i: (0, 0)),
+                  pl.BlockSpec(g2.shape, lambda i: (0, 0)),
                   pl.BlockSpec((None, d, TN), lambda i: (l, 0, clamp(i - nm_, nf_))),
                   pl.BlockSpec((None, d, TN), lambda i: (l, 0, clamp(i - nm_, nf_))),
                   pl.BlockSpec((None, TN, d), lambda i: (l, clamp(i - nm_, nf_), 0))]
@@ -359,10 +483,9 @@
         lq, g1, cos, sin, wq, wk, wv = qkv
         nq = wq.shape[2] // TN
         nq_ = nq
-        cs = pl.BlockSpec((seg, HEAD), lambda i: (qkv_half, 0))
-        qkv_half = 0
+        cs = pl.BlockSpec((seg, HEAD), lambda i: (hb, 0))
         args += [g1, cos, sin, wq, wk, wv]
-        specs += [pl.BlockSpec((1, d), lambda i: (0, 0)), cs, cs]
+        specs += [pl.BlockSpec(g1.shape, lambda i: (0, 0)), cs, cs]
         specs += [pl.BlockSpec((None, d, TN), lambda i, p=p: (lq, 0, clamp(i - base - p * nq_, nq_))) for p in (2, 1, 0)]
     if cache is not None:
         other, land = cache
@@ -389,7 +512,7 @@
     outs += [jax.ShapeDtypeStruct(a.shape, BF16) for a in send]
     ospecs += [HBM] * k
     out = pl.pallas_call(
-        functools.partial(_dense_kernel, ncp, nm, nf, nq, 2 * ncp if cache is not None else 0, k),
+        functools.partial(_dense_kernel, ncp, nm, nf, nq, l, lq, 2 * ncp if cache is not None else 0, k),
         grid=(nm + nf + 3 * nq,), in_specs=specs, out_specs=ospecs, out_shape=outs,
         scratch_shapes=scratch + _exchange_scratch(ncp, send), compiler_params=ids.params(k),
         name='dense' + ('_mlp' if nm else '') + ('_qkv' if nq else ''))(*args)
@@ -411,28 +534,21 @@
 
     def body(x, pos, g1, g2, wq, wk, wv, wo, w1, w3, w2):
         ids = _Ids()
-        seg = x.shape[0] // 2
         cos, sin = _angles(pos)
-        cl, sl, ch, sh = cos[:seg], sin[:seg], cos[seg:], sin[seg:]
-
-        def qkv(l, c, s):
-            return (l, g1[l:l + 1], c, s, wq, wk, wv)
 
         def mlp(l, o):
-            return (l, o, wo, g2[l:l + 1], w1, w3, w2)
-
+            return (l, o, wo, g2, w1, w3, w2)
+
+        qkv = (1, g1, cos, sin, wq, wk, wv)
         dense = functools.partial(_dense, ids, ncp)
-        a0l, _ = dense(x, 0, qkv=qkv(0, cl, sl))
-        a0h, (q, k0l, v0l) = dense(x, 1, qkv=qkv(0, ch, sh), send=a0l)
-        o, (v0h,) = _attention(ids, q, (k0l, v0l), send=(a0h[2],))
-        (o,) = _only(ids, ncp, (o,))
-        (xl, *a1l), (qh, k0h) = dense(x, 0, mlp=mlp(0, o), qkv=qkv(1, cl, sl), send=(a0h[0], a0h[1]))
-        oh, (q, k1l, v1l) = _attention(ids, qh, (k0l, v0l, k0h, v0h), send=tuple(a1l))
-        o, (oh,) = _attention(ids, q, (k1l, v1l), send=(oh,))
-        (xh, *a1h), (o,) = dense(x, 1, mlp=mlp(0, oh), qkv=qkv(1, ch, sh), send=(o,))
+        a0h, (q, k0l, v0l) = _first(ids, ncp, x, g1, cos, sin, wq, wk, wv)
+        o, _ = _attention(ids, q, (k0l, v0l))
+        (xl, *a1l), (q, k0h, v0h) = dense(x, 0, mlp=mlp(0, o), qkv=qkv, send=tuple(a0h))
+        o, (v1l,) = _attention(ids, q, (k0l, v0l, k0h, v0h), send=(a1l[2],))
+        (xh, *a1h), (q, k1l) = dense(x, 1, mlp=mlp(0, o), qkv=qkv, send=(a1l[0], a1l[1]))
+        o, _ = _attention(ids, q, (k1l, v1l))
         (xl,), (q, k1h, v1h) = dense(xl, None, mlp=mlp(1, o), send=tuple(a1h))
         o, _ = _attention(ids, q, (k1l, v1l, k1h, v1h))
-        (o,) = _only(ids, ncp, (o,))
         (y, kc, vc), _ = dense(xh, None, mlp=mlp(1, o), cache=(xl, (k0l, k1l, k0h, k1h, v0l, v1l, v0h, v1h)))
         return y, kc, vc
 

time: 648 us -> 526 us (0.81)
  the two profiles are of different devices: /device:TPU:112 before, /device:TPU:115 now
where the time goes in v2:
time: 526 us; the launch traced here: 518 us
  Pallas kernels  513 us (98%)
    pallas_call x4, Pallas kernels, _dense(): pl.pallas_call(functools.partial(_dense_kernel, ncp, nm, nf, nq, l, lq, 2...  289 us
    pallas_call x4, Pallas kernels, _attention(): pl.pallas_call(functools.partial(_attn_kernel, high, ncp, k), grid=(npair...  159 us
    pallas_call x1, Pallas kernels, _first(): pl.pallas_call(functools.partial(_first_kernel, ncp, nq), grid=(3 * nq,),...  65.4 us

profile of v2, /device:TPU:115, one launch (start us, length us, event | category | flops | bytes accessed | tf_op | source)
XLA Modules:
  0.0 517.9 jit_solution(14141003285513379250)
XLA Ops:
  0.6 0.7 convert_element_type.3
  1.3 1.4 fusion
  2.8 1.2 pad_maximum_fusion
  3.9 65.4 %first_qkv.1 = (bf16[8,384,256]{2,1,0:T(8,128)(2,1)}, bf16[8,384,256]{2,1,0:T(8,128)(2,1)}, bf16[8,384,256]{2,1,0:T(8,128)(2,1)}, bf16[8,384,256]{2,1,0:T(8,128)...) custom-call(bf16[768,2048]{1,0:T(8,128)(2,1)} %refs_0_.3, bf16[2,2048]{1,0:T(2,128)(2,1)} %refs_7_.3, ...), custom_call_target="tpu_custom_call" | custom-call | tf_op jit(solution)/shard_map/first_qkv/pallas_call | solution.py:323
  69.4 35.9 %attn_low.2.refs_1_ = bf16[8,384,256]{2,1,0:T(8,128)(2,1)} custom-call(bf16[3072,256]{1,0:T(8,128)(2,1)} %bitcast.27, bf16[3072,256]{1,0:T(8,128)(2,1)} %bitcast.12, bf16[3072,256]{1,0:T(8,128)(2,1)} %bitcast.14), custom_call_target="tpu_custom_call" | custom-call | tf_op jit(solution)/shard_map/attn_low/pallas_call | solution.py:236
  105.3 85.0 %dense_mlp_qkv.2 = (bf16[384,2048]{1,0:T(8,128)(2,1)}, bf16[8,384,256]{2,1,0:T(8,128)(2,1)}, bf16[8,384,256]{2,1,0:T(8,128)(2,1)}, bf16[8,384,256]{2,1,0:T(8,128...) custom-call(bf16[768,2048]{1,0:T(8,128)(2,1)} %refs_0_.3, ...), custom_call_target="tpu_custom_call" | custom-call | tf_op jit(solution)/shard_map/dense_mlp_qkv/pallas_call | solution.py:514
  190.2 44.9 %attn_high.2 = (bf16[8,384,256]{2,1,0:T(8,128)(2,1)}, bf16[8,384,256]{2,1,0:T(8,128)(2,1)}) custom-call(bf16[3072,256]{1,0:T(8,128)(2,1)} %bitcast.24, bf16[3072,256]{1,0:T(8,128)(2,1)} %bitcast.13, bf16[3072,256]{1,0:T(8,128)(2,1)} %bitcast.15, bf16[3072,256]{1,0:T(8,128)(2,1)} %bitcast.20, bf16[3072,256]{1,0:T(8,128)(2,1)} %bitcast.21, ...), custom_call_target="tpu_custom_call" | custom-call | tf_op jit(solution)/shard_map/attn_high/pallas_call | solution.py:236
  235.2 80.4 %dense_mlp_qkv.3 = (bf16[384,2048]{1,0:T(8,128)(2,1)}, bf16[8,384,256]{2,1,0:T(8,128)(2,1)}, bf16[8,384,256]{2,1,0:T(8,128)(2,1)}, bf16[8,384,256]{2,1,0:T(8,128...) custom-call(bf16[768,2048]{1,0:T(8,128)(2,1)} %refs_0_.3, ...), custom_call_target="tpu_custom_call" | custom-call | tf_op jit(solution)/shard_map/dense_mlp_qkv/pallas_call | solution.py:514
  315.6 32.9 %attn_low.3.refs_1_ = bf16[8,384,256]{2,1,0:T(8,128)(2,1)} custom-call(bf16[3072,256]{1,0:T(8,128)(2,1)} %bitcast.26, bf16[3072,256]{1,0:T(8,128)(2,1)} %bitcast.18, bf16[3072,256]{1,0:T(8,128)(2,1)} %bitcast.16), custom_call_target="tpu_custom_call" | custom-call | tf_op jit(solution)/shard_map/attn_low/pallas_call | solution.py:236
  348.5 61.9 %dense_mlp.2 = (bf16[384,2048]{1,0:T(8,128)(2,1)}, bf16[8,384,256]{2,1,0:T(8,128)(2,1)}, bf16[8,384,256]{2,1,0:T(8,128)(2,1)}, bf16[8,384,256]{2,1,0:T(8,128)(2,1)}) custom-call(bf16[384,2048]{1,0:T(8,128)(2,1)} %get-tuple-element.42.refs_0_, bf16[8,384,256]{2,1,0:T(8,128)(2,1)} %attn_low.3.refs_1_, bf16[2,2048,2048]{2,1,0:T(8,128)(2,1)} %refs_2_.7, ...), custom_call_target="tpu_custom_call" | custom-call | tf_op jit(solution)/shard_map/dense_mlp/pallas_call | solution.py:514
  410.4 45.1 %attn_high.3.refs_1_ = bf16[8,384,256]{2,1,0:T(8,128)(2,1)} custom-call(bf16[3072,256]{1,0:T(8,128)(2,1)} %bitcast.25, bf16[3072,256]{1,0:T(8,128)(2,1)} %bitcast.19, bf16[3072,256]{1,0:T(8,128)(2,1)} %bitcast.17, bf16[3072,256]{1,0:T(8,128)(2,1)} %bitcast.22, bf16[3072,256]{1,0:T(8,128)(2,1)} %bitcast.23), custom_call_target="tpu_custom_call" | custom-call | tf_op jit(solution)/shard_map/attn_high/pallas_call | solution.py:236
  455.5 62.0 %dense_mlp.3 = (bf16[768,2048]{1,0:T(8,128)(2,1)}, bf16[2,6144,2,128]{3,2,1,0:T(2,128)(2,1)}, bf16[2,6144,2,128]{3,2,1,0:T(2,128)(2,1)}) custom-call(bf16[384,2048]{1,0:T(8,128)(2,1)} %get-tuple-element.41.refs_0_, bf16[8,384,256]{2,1,0:T(8,128)(2,1)} %attn_high.3.refs_1_, bf16[2,2048,2048]{2,1,0:T(8,128)(2,1)} %refs_2_.7, bf16[2,2048]{1,0:T(2,128)(2,1)} %refs_3_.7, ...), custom_call_target="tpu_custom_call" | custom-call | tf_op jit(solution)/shard_map/dense_mlp/pallas_call | solution.py:514
  (1 shorter events, 0.0 us)

commit v3 on v2

--- a/solution.py
+++ b/solution.py
@@ -96,11 +96,22 @@
 EXTRA = 16
 
 
-def _attn_kernel(high, ncp, k, *refs):
+def _attn_kernel(high, ncp, nq, lq, k, *refs):
     nkv = 4 if high else 2
-    q_ref, kv, srcs = refs[0], refs[1:1 + nkv], refs[1 + nkv:1 + nkv + k]
-    land, dsts = refs[1 + nkv + k], refs[2 + nkv + k:2 + nkv + 2 * k]
-    sc = refs[2 + nkv + 2 * k:]
+    it = iter(refs)
+    take = lambda n: [next(it) for _ in range(n)]
+    q_ref, = take(1)
+    kv = take(nkv)
+    if nq:
+        x_ref, g1, cos, sin, wq, wk, wv = take(7)
+    srcs = take(k)
+    land, = take(1)
+    if nq:
+        qkv_out = take(3)
+    dsts = take(k)
+    if nq:
+        h_s, = take(1)
+    sc = list(it)
     s_s, m_s, acc, out, ssem, rsem, lsem = sc[:7]
     vt = sc[7:7 + nkv // 2]
     i = pl.program_id(0)
@@ -109,11 +120,12 @@
     c2 = 2 * seg
     npair = ncp // 2
     nh = w // HEAD
+    final = npair + 3 * nq - 1
     scale = HEAD ** -0.5 * LOG2E
     me = lax.axis_index('cp')
     req = lax.axis_index('req')
     b = lax.rem(me // 2 + 1 + i, npair)
-    ex = _Exchange(ncp, srcs, dsts, sc[7 + nkv // 2:], i == 0, i == 1, i == npair - 1) if k else None
+    ex = _Exchange(ncp, srcs, dsts, sc[7 + nkv // 2:], i == 0, i == 1, i == final) if k else None
 
     @pl.when(i == 0)
     def _():
@@ -129,9 +141,6 @@
                 for j in range(npair):
                     dst[h, :HEAD, j * c2:(j + 1) * c2] = src[j * c2:(j + 1) * c2, h * HEAD:(h + 1) * HEAD].T
                 dst[h, HEAD:, :] = jnp.ones((EXTRA, rows), BF16)
-
-    m_s[...] = jnp.full_like(m_s, -jnp.inf)
-    acc[...] = jnp.zeros_like(acc)
 
     def scores(kr, start, h):
         hs = slice(h * HEAD, (h + 1) * HEAD)
@@ -169,28 +178,36 @@
     def at(j):
         return (npair - 1 - j) * c2 if high else j * c2
 
-    if high:
-        scores(kv[0], 0, 0)
-        for j in range(npair):
-            if j + 1 < npair:
-                chunk(kv[0], vt[0], j * c2, kv[0], (j + 1) * c2)
-            else:
-                chunk(kv[0], vt[0], j * c2, kh, at(0))
+    def attend():
+        m_s[...] = jnp.full_like(m_s, -jnp.inf)
+        acc[...] = jnp.zeros_like(acc)
+        if high:
+            scores(kv[0], 0, 0)
+            for j in range(npair):
+                if j + 1 < npair:
+                    chunk(kv[0], vt[0], j * c2, kv[0], (j + 1) * c2)
+                else:
+                    chunk(kv[0], vt[0], j * c2, kh, at(0))
+        else:
+            scores(kh, 0, 0)
+
+        def body(j, _):
+            chunk(kh, vh, at(j), kh, at(j + 1))
+            return 0
+
+        lax.fori_loop(0, nb, body, 0)
+        for h in range(nh):
+            if h + 1 < nh:
+                scores(kh, b * c2, h + 1)
+            update(vh, b * c2, h, True)
+        for h in range(nh):
+            o = acc[h, :HEAD] / acc[h, HEAD:HEAD + 1]
+            out[i, :, h * HEAD:(h + 1) * HEAD] = o.T.astype(BF16)
+
+    if nq:
+        pl.when(i < npair)(attend)
     else:
-        scores(kh, 0, 0)
-
-    def body(j, _):
-        chunk(kh, vh, at(j), kh, at(j + 1))
-        return 0
-
-    lax.fori_loop(0, nb, body, 0)
-    for h in range(nh):
-        if h + 1 < nh:
-            scores(kh, b * c2, h + 1)
-        update(vh, b * c2, h, True)
-    for h in range(nh):
-        o = acc[h, :HEAD] / acc[h, HEAD:HEAD + 1]
-        out[i, :, h * HEAD:(h + 1) * HEAD] = o.T.astype(BF16)
+        attend()
 
     def send(step, pair, e):
         return pltpu.make_async_remote_copy(
@@ -202,17 +219,27 @@
         for e in range(2):
             send(i, b, e).start()
 
-    @pl.when(i == npair - 1)
-    def _():
-        mine = lax.rem(me, 2)
-        peer = 1 - mine
-        last = npair - 1
-        own = pltpu.make_async_copy(out.at[last, pl.ds(mine * seg, seg)], land.at[me], lsem)
+    mine = lax.rem(me, 2)
+    last = npair - 1
+    own = pltpu.make_async_copy(out.at[last, pl.ds(mine * seg, seg)], land.at[me], lsem)
+    twin = pltpu.make_async_remote_copy(
+        out.at[last, pl.ds((1 - mine) * seg, seg)], land.at[me], ssem.at[2 * last], rsem.at[2 * last],
+        device_id=(req, me + 1 - 2 * mine), device_id_type=MESH)
+
+    @pl.when(i == last)
+    def _():
         own.start()
-        twin = pltpu.make_async_remote_copy(
-            out.at[last, pl.ds(peer * seg, seg)], land.at[me], ssem.at[2 * last], rsem.at[2 * last],
-            device_id=(req, me + 1 - 2 * mine), device_id_type=MESH)
         twin.start()
+
+    if nq:
+        @pl.when(i == npair)
+        def _():
+            h_s[...] = _norm(x_ref[...], g1[lq:lq + 1])
+
+        _project(i - npair, nq, h_s, (wq, wk, wv), cos, sin, qkv_out)
+
+    @pl.when(i == final)
+    def _():
         for step in range(last):
             pair = lax.rem(me // 2 + 1 + step, npair)
             for e in range(2):
@@ -228,24 +255,39 @@
         ex.end()
 
 
-def _attention(ids, q, kv, send=()):
+def _attention(ids, q, kv, send=(), qkv=None):
     ncp, seg, w = q.shape
     high, nh, k = len(kv) == 4, w // HEAD, len(send)
     rows, c2, npair = ncp * seg, 2 * seg, ncp // 2
-    flat = pl.BlockSpec((rows, w), lambda i: (0, 0))
+    flat = pl.BlockSpec((rows, w), lambda i: (0, 0), pipeline_mode=pl.Buffered(1))
+    args, specs = [q.reshape(rows, w)] + [a.reshape(rows, w) for a in kv], [flat] * (1 + len(kv))
+    outs, ospecs, scratch, nq, lq = [jax.ShapeDtypeStruct(q.shape, BF16)], [HBM], [], 0, 0
+    if qkv is not None:
+        x, half, lq, g1, cos, sin, wq, wk, wv = qkv
+        d = x.shape[1]
+        nq = wq.shape[2] // TQ
+        clamp = lambda v, n: jnp.clip(v, 0, n - 1)
+        cs = pl.BlockSpec((seg, HEAD), lambda i: (half, 0))
+        args += [x, g1, cos, sin, wq, wk, wv]
+        specs += [pl.BlockSpec((seg, d), lambda i: (0, 0)), pl.BlockSpec(g1.shape, lambda i: (0, 0)), cs, cs]
+        specs += [pl.BlockSpec((None, d, TQ), lambda i, p=p: (lq, 0, clamp(i - npair - p * nq, nq))) for p in (2, 1, 0)]
+        outs += [jax.ShapeDtypeStruct((ncp, seg, w), BF16)] * 3
+        ospecs += [pl.BlockSpec((TQ // w, seg, w), lambda i, p=p: (clamp(i - npair - p * nq, nq), 0, 0)) for p in (2, 1, 0)]
+        scratch = [pltpu.VMEM((seg, d), BF16)]
     out = pl.pallas_call(
-        functools.partial(_attn_kernel, high, ncp, k),
-        grid=(npair,),
-        in_specs=[flat] * (1 + len(kv)) + [HBM] * k,
-        out_specs=[HBM] * (1 + k),
-        out_shape=[jax.ShapeDtypeStruct(a.shape, BF16) for a in (q,) + tuple(send)],
-        scratch_shapes=[pltpu.VMEM((nh, c2, c2), F32), pltpu.VMEM((nh, 1, c2), F32), pltpu.VMEM((nh, HEAD + EXTRA, c2), F32),
-                        pltpu.VMEM((npair, c2, w), BF16), pltpu.SemaphoreType.DMA((ncp,)), pltpu.SemaphoreType.DMA((ncp,)),
-                        pltpu.SemaphoreType.DMA]
+        functools.partial(_attn_kernel, high, ncp, nq, lq, k),
+        grid=(npair + 3 * nq,),
+        in_specs=specs + [HBM] * k,
+        out_specs=ospecs + [HBM] * k,
+        out_shape=outs + [jax.ShapeDtypeStruct(a.shape, BF16) for a in send],
+        scratch_shapes=scratch
+        + [pltpu.VMEM((nh, c2, c2), F32), pltpu.VMEM((nh, 1, c2), F32), pltpu.VMEM((nh, HEAD + EXTRA, c2), F32),
+           pltpu.VMEM((npair, c2, w), BF16), pltpu.SemaphoreType.DMA((ncp,)), pltpu.SemaphoreType.DMA((ncp,)),
+           pltpu.SemaphoreType.DMA]
         + [pltpu.VMEM((nh, HEAD + EXTRA, rows), BF16)] * (len(kv) // 2) + _exchange_scratch(ncp, send),
-        compiler_params=ids.params(True), name='attn_high' if high else 'attn_low',
-    )(q.reshape(rows, w), *[a.reshape(rows, w) for a in kv], *send)
-    return out[0], out[1:]
+        compiler_params=ids.params(True), name=('attn_high' if high else 'attn_low') + ('_qkv' if nq else ''),
+    )(*args, *send)
+    return out[:len(out) - k], out[len(out) - k:]
 
 
 def _first_kernel(ncp, nq, x_ref, g1, cos, sin, wq, wk, wv, qh, kh, vh, ql, kl, vl, h_s, buf, ssem, rsem, lsem):
@@ -332,6 +374,9 @@
     return out[:3], out[3:]
 
 
+TO = 512
+TF = 512
+TQ = 1024
 TN = 512
 
 
@@ -378,7 +423,7 @@
         for j in range(nm):
             @pl.when(i == j)
             def _():
-                ns = slice(j * TN, (j + 1) * TN)
+                ns = slice(j * TO, (j + 1) * TO)
                 x_s[:, ns] = (x_ref[:, ns].astype(F32) + jnp.dot(
                     o_s[...], wo[...], preferred_element_type=F32)).astype(BF16)
 
@@ -413,27 +458,7 @@
         def _():
             h_s[...] = _norm(x_s[...], g1[lq:lq + 1])
 
-        def project(w, out, rope):
-            t = jnp.dot(h_s[...], w[...], preferred_element_type=F32)
-            wd = out.shape[2]
-            for j in range(TN // HEAD):
-                th = t[:, j * HEAD:(j + 1) * HEAD]
-                if rope:
-                    th = th * cos[...] + pltpu.roll(th, HEAD // 2, 1) * sin[...]
-                lo = j * HEAD % wd
-                out[j * HEAD // wd, :, lo:lo + HEAD] = th.astype(BF16)
-
-        @pl.when((s >= 0) & (s < nq))
-        def _():
-            project(wv, vo, False)
-
-        @pl.when((s >= nq) & (s < 2 * nq))
-        def _():
-            project(wk, ko, True)
-
-        @pl.when(s >= 2 * nq)
-        def _():
-            project(wq, qo, True)
+        _project(s, nq, h_s, (wq, wk, wv), cos, sin, (qo, ko, vo))
     if cache:
         s = i - nm
         half = cache // 2
@@ -463,37 +488,39 @@
     k = len(send)
     nm = nf = nq = l = lq = 0
     clamp = lambda v, n: jnp.clip(v, 0, n - 1)
-    xs = pl.BlockSpec((seg, d), lambda i: (hb, 0))
+    one = dict(pipeline_mode=pl.Buffered(1))
+    xs = pl.BlockSpec((seg, d), lambda i: (hb, 0), **one)
     args, specs, outs, ospecs, scratch = [x], [xs], [], [], [pltpu.VMEM((seg, d), BF16)]
     if mlp is not None:
         l, o, wo, g2, w1, w3, w2 = mlp
         ff = w1.shape[2]
-        nm, nf = d // TN, ff // TN
+        tf = 2 * TF if qkv is None and cache is None else TF
+        nm, nf = d // TO, ff // tf
         nm_, nf_ = nm, nf
         args += [o, wo, g2, w1, w3, w2]
-        specs += [pl.BlockSpec(o.shape, lambda i: (0, 0, 0)),
-                  pl.BlockSpec((None, d, TN), lambda i: (l, 0, clamp(i, nm_))),
+        specs += [pl.BlockSpec(o.shape, lambda i: (0, 0, 0), **one),
+                  pl.BlockSpec((None, d, TO), lambda i: (l, 0, clamp(i, nm_))),
                   pl.BlockSpec(g2.shape, lambda i: (0, 0)),
-                  pl.BlockSpec((None, d, TN), lambda i: (l, 0, clamp(i - nm_, nf_))),
-                  pl.BlockSpec((None, d, TN), lambda i: (l, 0, clamp(i - nm_, nf_))),
-                  pl.BlockSpec((None, TN, d), lambda i: (l, clamp(i - nm_, nf_), 0))]
+                  pl.BlockSpec((None, d, tf), lambda i: (l, 0, clamp(i - nm_, nf_))),
+                  pl.BlockSpec((None, d, tf), lambda i: (l, 0, clamp(i - nm_, nf_))),
+                  pl.BlockSpec((None, tf, d), lambda i: (l, clamp(i - nm_, nf_), 0))]
         scratch += [pltpu.VMEM((seg, d), BF16), pltpu.VMEM((seg, d), BF16), pltpu.VMEM((seg, d), F32)]
     base = nm + nf
     if qkv is not None:
         lq, g1, cos, sin, wq, wk, wv = qkv
-        nq = wq.shape[2] // TN
+        nq = wq.shape[2] // TQ
         nq_ = nq
-        cs = pl.BlockSpec((seg, HEAD), lambda i: (hb, 0))
+        cs = pl.BlockSpec((seg, HEAD), lambda i: (hb, 0), **one)
         args += [g1, cos, sin, wq, wk, wv]
         specs += [pl.BlockSpec(g1.shape, lambda i: (0, 0)), cs, cs]
-        specs += [pl.BlockSpec((None, d, TN), lambda i, p=p: (lq, 0, clamp(i - base - p * nq_, nq_))) for p in (2, 1, 0)]
+        specs += [pl.BlockSpec((None, d, TQ), lambda i, p=p: (lq, 0, clamp(i - base - p * nq_, nq_))) for p in (2, 1, 0)]
     if cache is not None:
         other, land = cache
         w = land[0].shape[2]
         args += [other] + list(land)
         lo = pl.BlockSpec((None, seg, w), lambda i: (clamp(i - nm_, ncp), 0, 0))
         hi = pl.BlockSpec((None, seg, w), lambda i: (ncp - 1 - clamp(i - nm_ - ncp, ncp), 0, 0))
-        specs += [pl.BlockSpec((seg, d), lambda i: (0, 0))] + [lo, lo, hi, hi] * 2
+        specs += [pl.BlockSpec((seg, d), lambda i: (0, 0), **one)] + [lo, lo, hi, hi] * 2
     args += list(send)
     specs += [HBM] * k
     if mlp is not None:
@@ -504,7 +531,7 @@
         wd = wq.shape[2] // ncp
         for p in (2, 1, 0):
             outs.append(jax.ShapeDtypeStruct((ncp, seg, wd), BF16))
-            ospecs.append(pl.BlockSpec((TN // wd, seg, wd), lambda i, p=p: (clamp(i - base - p * nq_, nq_), 0, 0)))
+            ospecs.append(pl.BlockSpec((TQ // wd, seg, wd), lambda i, p=p: (clamp(i - base - p * nq_, nq_), 0, 0)))
     if cache is not None:
         for _ in range(2):
             outs.append(jax.ShapeDtypeStruct((2, 2 * ncp * seg, w // HEAD, HEAD), BF16))
@@ -519,6 +546,22 @@
     return out[:len(out) - k], out[len(out) - k:]
 
 
+def _project(s, nq, h_s, ws, cos, sin, outs):
+    def project(w, out, rope):
+        wd = out.shape[2]
+        t = jnp.dot(h_s[...], w[...], preferred_element_type=F32)
+        for c in range(0, TQ, HEAD):
+            th = t[:, c:c + HEAD]
+            if rope:
+                th = th * cos[...] + pltpu.roll(th, HEAD // 2, 1) * sin[...]
+            out[c // wd, :, c % wd:c % wd + HEAD] = th.astype(BF16)
+
+    for n, p in enumerate((2, 1, 0)):
+        @pl.when((s >= n * nq) & (s < (n + 1) * nq))
+        def _():
+            project(ws[p], outs[p], p < 2)
+
+
 def _angles(pos):
     half = HEAD // 2
     inv = 1.0 / (10000.0 ** (jnp.arange(half, dtype=F32) * (2.0 / HEAD)))
@@ -542,13 +585,13 @@
         qkv = (1, g1, cos, sin, wq, wk, wv)
         dense = functools.partial(_dense, ids, ncp)
         a0h, (q, k0l, v0l) = _first(ids, ncp, x, g1, cos, sin, wq, wk, wv)
-        o, _ = _attention(ids, q, (k0l, v0l))
+        (o,), _ = _attention(ids, q, (k0l, v0l))
         (xl, *a1l), (q, k0h, v0h) = dense(x, 0, mlp=mlp(0, o), qkv=qkv, send=tuple(a0h))
-        o, (v1l,) = _attention(ids, q, (k0l, v0l, k0h, v0h), send=(a1l[2],))
-        (xh, *a1h), (q, k1l) = dense(x, 1, mlp=mlp(0, o), qkv=qkv, send=(a1l[0], a1l[1]))
-        o, _ = _attention(ids, q, (k1l, v1l))
+        (o,), (v1l,) = _attention(ids, q, (k0l, v0l, k0h, v0h), send=(a1l[2],))
+        (xh,), (q, k1l) = dense(x, 1, mlp=mlp(0, o), send=(a1l[0], a1l[1]))
+        (o, *a1h), _ = _attention(ids, q, (k1l, v1l), qkv=(xh, 1) + qkv)
         (xl,), (q, k1h, v1h) = dense(xl, None, mlp=mlp(1, o), send=tuple(a1h))
-        o, _ = _attention(ids, q, (k1l, v1l, k1h, v1h))
+        (o,), _ = _attention(ids, q, (k1l, v1l, k1h, v1h))
         (y, kc, vc), _ = dense(xh, None, mlp=mlp(1, o), cache=(xl, (k0l, k1l, k0h, k1h, v0l, v1l, v0h, v1h)))
         return y, kc, vc
 

time: 526 us -> 508 us (0.966)
  the two profiles are of different devices: /device:TPU:115 before, /device:TPU:123 now
where the time goes in v3:
time: 508 us; the launch traced here: 500 us
  Pallas kernels  496 us (98%)
    pallas_call x4, Pallas kernels, _dense(): pl.pallas_call(functools.partial(_dense_kernel, ncp, nm, nf, nq, l, lq, 2...  263 us
    pallas_call x4, Pallas kernels, _attention(): pl.pallas_call(functools.partial(_attn_kernel, high, ncp, nq, lq, k), gri...  167 us
    pallas_call x1, Pallas kernels, _first(): pl.pallas_call(functools.partial(_first_kernel, ncp, nq), grid=(3 * nq,),...  65.4 us

profile of v3, /device:TPU:123, one launch (start us, length us, event | category | flops | bytes accessed | tf_op | source)
XLA Modules:
  0.0 500.3 jit_solution(4064815088249937630)
XLA Ops:
  0.6 0.7 convert_element_type.3
  1.3 1.4 fusion
  2.8 1.2 pad_maximum_fusion
  3.9 65.4 %first_qkv.1 = (bf16[8,384,256]{2,1,0:T(8,128)(2,1)}, bf16[8,384,256]{2,1,0:T(8,128)(2,1)}, bf16[8,384,256]{2,1,0:T(8,128)(2,1)}, bf16[8,384,256]{2,1,0:T(8,128)...) custom-call(bf16[768,2048]{1,0:T(8,128)(2,1)} %refs_0_.3, bf16[2,2048]{1,0:T(2,128)(2,1)} %refs_4_.7, ...), custom_call_target="tpu_custom_call" | custom-call | tf_op jit(solution)/shard_map/first_qkv/pallas_call | solution.py:365
  69.4 35.9 %attn_low.1.refs_1_ = bf16[8,384,256]{2,1,0:T(8,128)(2,1)} custom-call(bf16[3072,256]{1,0:T(8,128)(2,1)} %bitcast.26, bf16[3072,256]{1,0:T(8,128)(2,1)} %bitcast.12, bf16[3072,256]{1,0:T(8,128)(2,1)} %bitcast.14), custom_call_target="tpu_custom_call" | custom-call | tf_op jit(solution)/shard_map/attn_low/pallas_call | solution.py:277
  105.2 82.9 %dense_mlp_qkv.1 = (bf16[384,2048]{1,0:T(8,128)(2,1)}, bf16[8,384,256]{2,1,0:T(8,128)(2,1)}, bf16[8,384,256]{2,1,0:T(8,128)(2,1)}, bf16[8,384,256]{2,1,0:T(8,128...) custom-call(bf16[768,2048]{1,0:T(8,128)(2,1)} %refs_0_.3, ...), custom_call_target="tpu_custom_call" | custom-call | tf_op jit(solution)/shard_map/dense_mlp_qkv/pallas_call | solution.py:541
  188.1 45.0 %attn_high.2 = (bf16[8,384,256]{2,1,0:T(8,128)(2,1)}, bf16[8,384,256]{2,1,0:T(8,128)(2,1)}) custom-call(bf16[3072,256]{1,0:T(8,128)(2,1)} %bitcast.24, bf16[3072,256]{1,0:T(8,128)(2,1)} %bitcast.13, bf16[3072,256]{1,0:T(8,128)(2,1)} %bitcast.15, bf16[3072,256]{1,0:T(8,128)(2,1)} %bitcast.20, bf16[3072,256]{1,0:T(8,128)(2,1)} %bitcast.21, ...), custom_call_target="tpu_custom_call" | custom-call | tf_op jit(solution)/shard_map/attn_high/pallas_call | solution.py:277
  233.1 56.6 %dense_mlp.3 = (bf16[384,2048]{1,0:T(8,128)(2,1)}, bf16[8,384,256]{2,1,0:T(8,128)(2,1)}, bf16[8,384,256]{2,1,0:T(8,128)(2,1)}) custom-call(bf16[768,2048]{1,0:T(8,128)(2,1)} %refs_0_.3, bf16[8,384,256]{2,1,0:T(8,128)(2,1)} %get-tuple-element.39.refs_1_, bf16[2,2048,2048]{2,1,0:T(8,128)(2,1)} %refs_2_.7, bf16[2,2048]{1,0:T(2,128)(2,1)} %refs_3_.7, ...), custom_call_target="tpu_custom_call" | custom-call | tf_op jit(solution)/shard_map/dense_mlp/pallas_call | solution.py:541
  289.8 40.9 %attn_low_qkv.1 = (bf16[8,384,256]{2,1,0:T(8,128)(2,1)}, bf16[8,384,256]{2,1,0:T(8,128)(2,1)}, bf16[8,384,256]{2,1,0:T(8,128)(2,1)}, bf16[8,384,256]{2,1,0:T(8,128)(2,1)}) custom-call(bf16[3072,256]{1,0:T(8,128)(2,1)} %bitcast.27, bf16[3072,256]{1,0:T(8,128)(2,1)} %bitcast.18, bf16[3072,256]{1,0:T(8,128)(2,1)} %bitcast.16, ...), custom_call_target="tpu_custom_call" | custom-call | tf_op jit(solution)/shard_map/attn_low_qkv/pallas_call | solution.py:277
  330.7 61.7 %dense_mlp.4 = (bf16[384,2048]{1,0:T(8,128)(2,1)}, bf16[8,384,256]{2,1,0:T(8,128)(2,1)}, bf16[8,384,256]{2,1,0:T(8,128)(2,1)}, bf16[8,384,256]{2,1,0:T(8,128)(2,1)}) custom-call(bf16[384,2048]{1,0:T(8,128)(2,1)} %get-tuple-element.43.refs_0_, bf16[8,384,256]{2,1,0:T(8,128)(2,1)} %get-tuple-element.47.refs_1_, bf16[2,2048,2048]{2,1,0:T(8,128)(2,1)} %refs_2_.7, ...), custom_call_target="tpu_custom_call" | custom-call | tf_op jit(solution)/shard_map/dense_mlp/pallas_call | solution.py:541
  392.4 45.5 %attn_high.3.refs_1_ = bf16[8,384,256]{2,1,0:T(8,128)(2,1)} custom-call(bf16[3072,256]{1,0:T(8,128)(2,1)} %bitcast.25, bf16[3072,256]{1,0:T(8,128)(2,1)} %bitcast.19, bf16[3072,256]{1,0:T(8,128)(2,1)} %bitcast.17, bf16[3072,256]{1,0:T(8,128)(2,1)} %bitcast.22, bf16[3072,256]{1,0:T(8,128)(2,1)} %bitcast.23), custom_call_target="tpu_custom_call" | custom-call | tf_op jit(solution)/shard_map/attn_high/pallas_call | solution.py:277
  437.9 62.2 %dense_mlp.5 = (bf16[768,2048]{1,0:T(8,128)(2,1)}, bf16[2,6144,2,128]{3,2,1,0:T(2,128)(2,1)}, bf16[2,6144,2,128]{3,2,1,0:T(2,128)(2,1)}) custom-call(bf16[384,2048]{1,0:T(8,128)(2,1)} %get-tuple-element.42.refs_3_.refs_0_, bf16[8,384,256]{2,1,0:T(8,128)(2,1)} %attn_high.3.refs_1_, bf16[2,2048,2048]{2,1,0:T(8,128)(2,1)} %refs_2_.7, bf16[2,2048]{1,0:T(2,128)(2,1)} %refs_3_.7, ...), custom_call_target="tpu_custom_call" | custom-call | tf_op jit(solution)/shard_map/dense_mlp/pallas_call | solution.py:541
  (1 shorter events, 0.0 us)
